TPU v7x, 512 devices: a whole 4x8x8 slice. The times are simulated.
512 devices in a mesh: row: 32 (over z, y_hi, core), col: 16 (over y_lo, x).
Axes of the slice: x: 4, y: 8 (y_hi: 2, y_lo: 4; y = y_hi * 4 + y_lo), z: 8, core: 2. Of those that a mesh axis runs over, the one named last changes fastest.
Arguments:
- energy: float32 [16, 2048, 2048], P('col', 'row'), may hold values from 0.5 to 8
- damage_old: float32 [16, 2048, 2048], P('col', 'row'), may hold values from 0 to 0.8
- crack_seeds: int32 [16, 2048, 2048], P('col', 'row'), may hold values 0 or 1
- irreversible: int32 [16, 2048, 2048], P('col', 'row'), may hold values 0 or 1
- line_inverses: float32 [8, 256, 256], replicated, may hold values from -0.6 to 2.8
- z_inverse: float32 [16, 16], replicated, may hold values from -0.8 to 1.9
Outputs:
- damage: float32 [16, 2048, 2048], P('col', 'row')
- update_norms: float32 [2], replicated
All inputs are finite; a program needn't handle non-finite values. No bound on the sum of `crack_seeds` or of `irreversible` on one device may be relied on, other than what follows from the above.
Results may differ from a plain program's by a relative error of at most 0.0001.
Values sent between devices are 32-bit elements; how exact they have to be, the bound alone decides.
No kernel may reach another device: no remote copies, remote signals or barrier semaphores. Data moves between devices by JAX's collectives and lax.ppermute only.
A program may use at most 64 MiB of HBM per device.

v0:
```python
import jax
import jax.numpy as jnp
from jax import lax
from jax.experimental import pallas as pl
from jax.experimental.pallas import tpu as pltpu
from jax.sharding import Mesh
from jax.sharding import PartitionSpec as P

ROW = ("row_0", "row_1", "row_2")
COL = ("col_0", "col_1")
ALL = ROW + COL

KAPPA = 2.0
STEP = 0.02
COUPLE = 0.5
EPSILON = 1e-06
HALF = 64


def iota(shape, axis):
    return lax.broadcasted_iota(jnp.int32, shape, axis)


def lane_lap(field):
    extent = field.shape[1]
    lane = iota(field.shape, 1)
    ahead = jnp.where(lane == extent - 1, field, pltpu.roll(field, extent - 1, 1))
    behind = jnp.where(lane == 0, field, pltpu.roll(field, 1, 1))
    return (ahead - field) + (behind - field)


def plane_lap(field, planes):
    extent = field.shape[0]
    plane = iota(field.shape, 0) % planes
    ahead = jnp.where(plane == planes - 1, field, pltpu.roll(field, extent - 1, 0))
    behind = jnp.where(plane == 0, field, pltpu.roll(field, 1, 0))
    return (ahead - field) + (behind - field)


def line_solve(lines, inverses_ref):
    count = lines.shape[0]
    blocks, cells, _ = inverses_ref.shape
    unit_row = iota((8, cells), 0)
    unit_lane = iota((8, cells), 1)
    units = jnp.where(
        ((unit_row == 0) & (unit_lane == 0)) | ((unit_row == 1) & (unit_lane == cells - 1)), 1.0, 0.0
    )
    products, firsts, lasts = [], [], []
    for k in range(blocks):
        stacked = jnp.concatenate([lines[:, k * cells : (k + 1) * cells], units], axis=0)
        result = lax.dot_general(
            stacked,
            inverses_ref[k],
            (((1,), (1,)), ((), ())),
            precision=lax.Precision.HIGHEST,
            preferred_element_type=jnp.float32,
        )
        products.append(result[:count])
        firsts.append(result[count : count + 1])
        lasts.append(result[count + 1 : count + 2])
    inflow = [jnp.zeros((count, 1), jnp.float32)]
    heads = []
    for k in range(blocks):
        heads.append(products[k][:, 0:1] + COUPLE * inflow[k] * firsts[k][:, 0:1])
        if k < blocks - 1:
            inflow.append(
                products[k][:, cells - 1 : cells] + COUPLE * inflow[k] * firsts[k][:, cells - 1 : cells]
            )
    outflow = [None] * blocks
    carried = heads[blocks - 1]
    for k in range(blocks - 2, -1, -1):
        outflow[k] = carried
        carried = heads[k] + COUPLE * carried * lasts[k][:, 0:1]
    solved = []
    for k in range(blocks):
        value = products[k]
        if k > 0:
            value = value + (COUPLE * inflow[k]) * firsts[k]
        if k < blocks - 1:
            value = value + (COUPLE * outflow[k]) * lasts[k]
        solved.append(value)
    return jnp.concatenate(solved, axis=1)


def send_rows(out_ref, field, first, stride):
    chunks = field.shape[1] // 4
    for s in range(2):
        pair = jnp.concatenate(
            [field[:, 2 * s * chunks : (2 * s + 1) * chunks], field[:, (2 * s + 1) * chunks : (2 * s + 2) * chunks]],
            axis=0,
        )
        out_ref[pl.ds(first + s, chunks, stride=stride), :] = pair.T


def receive_rows(in_ref):
    chunks = in_ref.shape[0] // 2
    parts = []
    for s in range(2):
        pair = in_ref[pl.ds(s, chunks, stride=2), :].T
        parts.append(pair[:HALF])
        parts.append(pair[HALF:])
    return jnp.concatenate(parts, axis=1)


def partial_residual(energy, damage):
    return energy - (1.0 + energy) * damage + KAPPA * lane_lap(damage)


def first_kernel(energy_ref, old_ref, seeds_ref, out_ref):
    energy = energy_ref[0]
    damage = jnp.where(seeds_ref[0] == 1, 1.0, old_ref[0])
    send_rows(out_ref, damage, 2, 4)
    send_rows(out_ref, partial_residual(energy, damage), 0, 4)


def cross_kernel(in_ref, inverses_ref, z_ref, out_ref):
    planes = z_ref.shape[0]
    rows = in_ref.shape[0] // (4 * planes)
    low = iota((planes, 2 * HALF), 1) < HALF

    def gather(first):
        lines = [[], [], [], []]
        for j in range(rows // 2):
            for s in range(2):
                even = in_ref[pl.ds(2 * j * 4 * planes + first + s, planes, stride=4), :]
                odd = in_ref[pl.ds((2 * j + 1) * 4 * planes + first + s, planes, stride=4), :]
                lines[2 * s].append(jnp.where(low, even, pltpu.roll(odd, HALF, 1)))
                lines[2 * s + 1].append(jnp.where(low, pltpu.roll(even, HALF, 1), odd))
        return jnp.concatenate([jnp.concatenate(line, axis=1) for line in lines], axis=0)

    damage = gather(2)
    turned = gather(0) + KAPPA * (lane_lap(damage) + plane_lap(damage, planes))
    along_y = line_solve(turned, inverses_ref)
    wide = jnp.concatenate([z_ref[...]] * 4, axis=1)
    tiled = jnp.concatenate([wide] * 4, axis=0)
    same = iota(tiled.shape, 0) // planes == iota(tiled.shape, 1) // planes
    along_z = jnp.dot(
        jnp.where(same, tiled, 0.0),
        along_y,
        precision=lax.Precision.HIGHEST,
        preferred_element_type=jnp.float32,
    )
    for j in range(rows // 2):
        for s in range(2):
            first = along_z[2 * s * planes : (2 * s + 1) * planes, j * 128 : (j + 1) * 128]
            second = along_z[(2 * s + 1) * planes : (2 * s + 2) * planes, j * 128 : (j + 1) * 128]
            out_ref[pl.ds(2 * j * 2 * planes + s, planes, stride=2), :] = jnp.where(
                low, first, pltpu.roll(second, HALF, 1)
            )
            out_ref[pl.ds((2 * j + 1) * 2 * planes + s, planes, stride=2), :] = jnp.where(
                low, pltpu.roll(first, HALF, 1), second
            )


def renew(in_ref, damage, old, seeds, irreversible, inverses_ref):
    update = STEP * line_solve(receive_rows(in_ref), inverses_ref)
    lower_bound = jnp.where(irreversible == 1, old, 0.0)
    clamped = jnp.minimum(jnp.maximum(damage + update, lower_bound), 1.0)
    renewed = jnp.where(seeds == 1, 1.0, clamped)
    change = jnp.sum((renewed - damage) ** 2)
    return renewed, change


def middle_kernel(
    in_ref, energy_ref, old_ref, seeds_ref, irreversible_ref, inverses_ref, out_ref, damage_ref, change_ref
):
    old = old_ref[0]
    seeds = seeds_ref[0]
    damage = jnp.where(seeds == 1, 1.0, old)
    renewed, change = renew(in_ref, damage, old, seeds, irreversible_ref[0], inverses_ref)
    damage_ref[0] = renewed
    send_rows(out_ref, renewed, 2, 4)
    send_rows(out_ref, partial_residual(energy_ref[0], renewed), 0, 4)
    change_ref[...] = jnp.full(change_ref.shape, change, jnp.float32)


def last_kernel(
    in_ref, damage_in_ref, old_ref, seeds_ref, irreversible_ref, inverses_ref, first_change_ref, damage_ref, change_ref
):
    renewed, change = renew(
        in_ref, damage_in_ref[0], old_ref[0], seeds_ref[0], irreversible_ref[0], inverses_ref
    )
    damage_ref[0] = renewed
    lane = iota(change_ref.shape, 1)
    change_ref[...] = jnp.where(lane == 0, first_change_ref[...], jnp.where(lane == 1, change, 0.0))


def call(kernel, outs, *args):
    return pl.pallas_call(
        kernel,
        out_shape=[jax.ShapeDtypeStruct(shape, jnp.float32) for shape in outs],
        in_specs=[pl.BlockSpec(memory_space=pltpu.VMEM) for _ in args],
        out_specs=[pl.BlockSpec(memory_space=pltpu.VMEM) for _ in outs],
        compiler_params=pltpu.CompilerParams(vmem_limit_bytes=48 * 1024 * 1024),
    )(*args)


def exchange(rows):
    return lax.all_to_all(rows, ALL, split_axis=0, concat_axis=0, tiled=True)


def local(energy, damage_old, crack_seeds, irreversible, line_inverses, z_inverse):
    planes, rows_here, line_length = energy.shape
    devices = lax.axis_size(ALL)
    cell_count = planes * rows_here * line_length * devices
    one = planes * rows_here * line_length // 128
    (sent,) = call(first_kernel, [(2 * one, 128)], energy, damage_old, crack_seeds)
    (crossed,) = call(cross_kernel, [(one, 128)], exchange(sent), line_inverses, z_inverse)
    sent, damage, change = call(
        middle_kernel,
        [(2 * one, 128), energy.shape, (1, 128)],
        exchange(crossed),
        energy,
        damage_old,
        crack_seeds,
        irreversible,
        line_inverses,
    )
    (crossed,) = call(cross_kernel, [(one, 128)], exchange(sent), line_inverses, z_inverse)
    damage, change = call(
        last_kernel,
        [energy.shape, (1, 128)],
        exchange(crossed),
        damage,
        damage_old,
        crack_seeds,
        irreversible,
        line_inverses,
        change,
    )
    every = exchange(jnp.broadcast_to(change, (devices, 128)))
    global_sums = jnp.sum(every, axis=0)[:2]
    update_norms = jnp.sqrt(global_sums / cell_count + EPSILON) / STEP
    return (damage, update_norms)


def solution(mesh):
    finer = Mesh(mesh.devices.reshape(8, 2, 2, 4, 4), ALL)
    spec = P(COL, ROW, None)
    in_specs = (spec, spec, spec, spec, P(), P())
    return jax.shard_map(local, mesh=finer, in_specs=in_specs, out_specs=(spec, P()), check_vma=False)
```

profile of v0, /device:TPU:1, one launch (start us, length us, event | category | flops | bytes accessed | tf_op | source)
XLA Modules:
  0.0 205.2 jit_solution(4920342528060660510)
XLA Ops:
  0.6 0.0 copy-start
  0.6 0.0 copy-start.2
  0.7 1.2 copy-done.2
  1.8 0.0 copy-start.4
  1.8 1.0 copy-done.4
  2.9 0.0 copy-start.5
  2.9 1.0 copy-done.5
  3.9 0.0 copy-start.8
  3.9 0.6 shard_map.77
  4.6 56.0 %all_to_all.50 = f32[512,4,128]{2,1,0:T(4,128)S(1)} all-to-all(f32[512,4,128]{2,1,0:T(4,128)S(1)} %bitcast.12), channel_id=1, replica_groups=mesh['row_0'=8,'row_1'=2,'row_2'=2,'col_0'=4,'col_1'=4] {'row_0','row_1'..., dimensions={0} | all-to-all | bytes 2097152 | tf_op jit(solution)/shard_map/all_to_all | solution.py:199
  60.6 0.0 copy-done
  60.6 0.0 copy-done.8
  60.6 0.0 copy-start.3
  60.6 0.0 copy-start.6
  60.6 0.0 copy-start.7
  60.6 3.2 %shard_map.78 = f32[1024,128]{1,0:T(8,128)S(1)} custom-call(f32[2048,128]{1,0:T(8,128)S(1)} %bitcast.10, f32[8,256,256]{2,1,0:T(8,128)S(1)} %copy-done, f32[16,16]{1,0:T(8,128)S(1)} %copy-done.8), custom_call_target="tpu_custom_call" | custom-call | tf_op jit(solution)/shard_map/pallas_call | solution.py:189
  63.9 30.3 %all_to_all.51 = f32[512,2,128]{2,1,0:T(2,128)S(1)} all-to-all(f32[512,2,128]{2,1,0:T(2,128)S(1)} %bitcast.15), channel_id=1, replica_groups=mesh['row_0'=8,'row_1'=2,'row_2'=2,'col_0'=4,'col_1'=4] {'row_0','row_1'..., dimensions={0} | all-to-all | bytes 1048576 | tf_op jit(solution)/shard_map/all_to_all | solution.py:199
  94.1 0.0 copy-done.3
  94.1 0.0 copy-done.6
  94.2 0.0 copy-done.7
  94.2 4.4 %shard_map.79 = (f32[2048,128]{1,0:T(8,128)S(1)}, f32[1,64,2048]{2,1,0:T(8,128)S(1)}, f32[1,128]{1,0:T(1,128)S(1)}) custom-call(f32[1024,128]{1,0:T(8,128)S(1)} %bitcast.14, f32[1,64,2048]{2,1,0:T(8,128)S(1)} %copy-done.6, f32[1,64,2048]{2,1,0:T(8,128)S(1)} %copy-done.3, s32[1,64,2048]{2,1,0:T(8,128)S(1)} %copy-done.4, s32[1,64,2048]{2,1,0:T(8,128)S(1)} %copy-done.7, ...), custom_call_target="tpu_custom_call" | custom-call | tf_op jit(solution)/shard_map/pallas_call | solution.py:189
  98.5 0.0 copy-start.1
  98.5 43.0 %all_to_all.52 = f32[512,4,128]{2,1,0:T(4,128)S(1)} all-to-all(f32[512,4,128]{2,1,0:T(4,128)S(1)} %bitcast.17), channel_id=1, replica_groups=mesh['row_0'=8,'row_1'=2,'row_2'=2,'col_0'=4,'col_1'=4] {'row_0','row_1'..., dimensions={0} | all-to-all | bytes 2097152 | tf_op jit(solution)/shard_map/all_to_all | solution.py:199
  141.5 0.0 copy-done.1
  141.5 3.2 %shard_map.80 = f32[1024,128]{1,0:T(8,128)S(1)} custom-call(f32[2048,128]{1,0:T(8,128)S(1)} %bitcast.11, f32[8,256,256]{2,1,0:T(8,128)S(1)} %copy-done.1, f32[16,16]{1,0:T(8,128)S(1)} %copy-done.8), custom_call_target="tpu_custom_call" | custom-call | tf_op jit(solution)/shard_map/pallas_call | solution.py:189
  144.8 30.3 %all_to_all.53 = f32[512,2,128]{2,1,0:T(2,128)S(1)} all-to-all(f32[512,2,128]{2,1,0:T(2,128)S(1)} %bitcast.16), channel_id=1, replica_groups=mesh['row_0'=8,'row_1'=2,'row_2'=2,'col_0'=4,'col_1'=4] {'row_0','row_1'..., dimensions={0} | all-to-all | bytes 1048576 | tf_op jit(solution)/shard_map/all_to_all | solution.py:199
  175.1 3.2 %shard_map.81 = (f32[1,64,2048]{2,1,0:T(8,128)}, f32[1,128]{1,0:T(1,128)S(1)}) custom-call(f32[1024,128]{1,0:T(8,128)S(1)} %bitcast.13, f32[1,64,2048]{2,1,0:T(8,128)S(1)} %get-tuple-element.8.damage_in_ref, f32[1,64,2048]{2,1,0:T(8,128)S(1)} %copy-done.3, s32[1,64,2048]{2,1,0:T(8,128)S(1)} %copy-done.4, s32[1,64,2048]{2,1,0:T(8,128)S(1)} %copy-done.7, ...), custom_call_target="tpu_custom_call" | custom-call | tf_op jit(solution)/shard_map/pallas_call | solution.py:189
  178.3 0.1 broadcast_in_dim.2
  178.4 26.2 %all_to_all.54 = f32[512,1,128]{2,1,0:T(1,128)S(1)} all-to-all(f32[512,1,128]{2,1,0:T(1,128)S(1)} %broadcast_in_dim.2), channel_id=1, replica_groups=mesh['row_0'=8,'row_1'=2,'row_2'=2,'col_0'=4,'col_1'=4] {'row_0','row_1'..., dimensions={0} | all-to-all | bytes 524288 | tf_op jit(solution)/shard_map/all_to_all | solution.py:199
  204.6 0.1 reduce_sum.9
  204.7 0.5 sqrt_multiply_fusion
Async XLA Ops:
  0.6 60.0 %copy-start = (f32[8,256,256]{2,1,0:T(8,128)S(1)}, f32[8,256,256]{2,1,0:T(8,128)}, u32[]{:S(2)}) copy-start(f32[8,256,256]{2,1,0:T(8,128)} %inverses_ref.7) | copy-start | bytes 6291460
  0.6 1.2 copy-start.2
  1.8 1.0 copy-start.4
  2.9 1.0 copy-start.5
  3.9 56.7 %copy-start.8 = (f32[16,16]{1,0:T(8,128)S(1)}, f32[16,16]{1,0:T(8,128)}, u32[]{:S(2)}) copy-start(f32[16,16]{1,0:T(8,128)} %z_ref.3) | copy-start | bytes 3076
  60.6 33.6 %copy-start.3 = (f32[1,64,2048]{2,1,0:T(8,128)S(1)}, f32[1,64,2048]{2,1,0:T(8,128)}, u32[]{:S(2)}) copy-start(f32[1,64,2048]{2,1,0:T(8,128)} %old_ref.5) | copy-start | bytes 1572868
  60.6 33.6 %copy-start.6 = (f32[1,64,2048]{2,1,0:T(8,128)S(1)}, f32[1,64,2048]{2,1,0:T(8,128)}, u32[]{:S(2)}) copy-start(f32[1,64,2048]{2,1,0:T(8,128)} %energy_ref.3) | copy-start | bytes 1572868
  60.6 33.6 %copy-start.7 = (s32[1,64,2048]{2,1,0:T(8,128)S(1)}, s32[1,64,2048]{2,1,0:T(8,128)}, u32[]{:S(2)}) copy-start(s32[1,64,2048]{2,1,0:T(8,128)} %irreversible_ref.3) | copy-start | bytes 1572868
  98.5 43.0 %copy-start.1 = (f32[8,256,256]{2,1,0:T(8,128)S(1)}, f32[8,256,256]{2,1,0:T(8,128)}, u32[]{:S(2)}) copy-start(f32[8,256,256]{2,1,0:T(8,128)} %inverses_ref.7) | copy-start | bytes 6291460
where the time goes:
time: 206 us; the launch traced here: 205 us
  blocking collectives  186 us (90%)
  Pallas kernels  14.7 us (7%)
  local copies, waits for them, and re-layouts  3.43 us (2%)
    all_to_all x5, blocking collectives, exchange(): return lax.all_to_all(rows, ALL, split_axis=0, concat_axis=0, tiled=True)  186 us
    pallas_call x5, Pallas kernels, call(): pl.pallas_call(kernel, out_shape=[jax.ShapeDtypeStruct(shape, jnp.float32...  14.7 us

commit v1 on v0

v1 whole, which is shorter than its diff:
```python
import jax
import jax.numpy as jnp
from jax import lax
from jax.experimental import pallas as pl
from jax.experimental.pallas import tpu as pltpu
from jax.sharding import Mesh
from jax.sharding import PartitionSpec as P

ROW = ("row_0", "row_1", "row_2")
COL = ("col_0", "col_1")
ALL = ROW + COL
PLANE = ROW[1:] + COL

ITERS = 2

KAPPA = 2.0
STEP = 0.02
COUPLE = 0.5
EPSILON = 1e-06
HALF = 64


def iota(shape, axis):
    return lax.broadcasted_iota(jnp.int32, shape, axis)


def lane_lap(field):
    extent = field.shape[1]
    lane = iota(field.shape, 1)
    ahead = jnp.where(lane == extent - 1, field, pltpu.roll(field, extent - 1, 1))
    behind = jnp.where(lane == 0, field, pltpu.roll(field, 1, 1))
    return (ahead - field) + (behind - field)


def plane_lap(field, planes):
    extent = field.shape[0]
    plane = iota(field.shape, 0) % planes
    ahead = jnp.where(plane == planes - 1, field, pltpu.roll(field, extent - 1, 0))
    behind = jnp.where(plane == 0, field, pltpu.roll(field, 1, 0))
    return (ahead - field) + (behind - field)


def line_solve(lines, inverses_ref):
    count = lines.shape[0]
    blocks, cells, _ = inverses_ref.shape
    unit_row = iota((8, cells), 0)
    unit_lane = iota((8, cells), 1)
    units = jnp.where(
        ((unit_row == 0) & (unit_lane == 0)) | ((unit_row == 1) & (unit_lane == cells - 1)), 1.0, 0.0
    )
    products, firsts, lasts = [], [], []
    for k in range(blocks):
        stacked = jnp.concatenate([lines[:, k * cells : (k + 1) * cells], units], axis=0)
        result = lax.dot_general(
            stacked,
            inverses_ref[k],
            (((1,), (1,)), ((), ())),
            precision=lax.Precision.HIGHEST,
            preferred_element_type=jnp.float32,
        )
        products.append(result[:count])
        firsts.append(result[count : count + 1])
        lasts.append(result[count + 1 : count + 2])
    inflow = [jnp.zeros((count, 1), jnp.float32)]
    heads = []
    for k in range(blocks):
        heads.append(products[k][:, 0:1] + COUPLE * inflow[k] * firsts[k][:, 0:1])
        if k < blocks - 1:
            inflow.append(
                products[k][:, cells - 1 : cells] + COUPLE * inflow[k] * firsts[k][:, cells - 1 : cells]
            )
    outflow = [None] * blocks
    carried = heads[blocks - 1]
    for k in range(blocks - 2, -1, -1):
        outflow[k] = carried
        carried = heads[k] + COUPLE * carried * lasts[k][:, 0:1]
    solved = []
    for k in range(blocks):
        value = products[k]
        if k > 0:
            value = value + (COUPLE * inflow[k]) * firsts[k]
        if k < blocks - 1:
            value = value + (COUPLE * outflow[k]) * lasts[k]
        solved.append(value)
    return jnp.concatenate(solved, axis=1)


def send_rows(out_ref, field, first, stride):
    chunks = field.shape[1] // 4
    for s in range(2):
        pair = jnp.concatenate(
            [field[:, 2 * s * chunks : (2 * s + 1) * chunks], field[:, (2 * s + 1) * chunks : (2 * s + 2) * chunks]],
            axis=0,
        )
        out_ref[pl.ds(first + s, chunks, stride=stride), :] = pair.T


def receive_rows(in_ref, first, stride):
    chunks = in_ref.shape[0] // stride
    parts = []
    for s in range(2):
        pair = in_ref[pl.ds(first + s, chunks, stride=stride), :].T
        parts.append(pair[:HALF])
        parts.append(pair[HALF:])
    return jnp.concatenate(parts, axis=1)


def gather_lines(in_ref, planes, first, stride):
    rows = in_ref.shape[0] // (stride * planes)
    low = iota((planes, 2 * HALF), 1) < HALF
    lines = [[], [], [], []]
    for j in range(rows // 2):
        for s in range(2):
            even = in_ref[pl.ds(2 * j * stride * planes + first + s, planes, stride=stride), :]
            odd = in_ref[pl.ds((2 * j + 1) * stride * planes + first + s, planes, stride=stride), :]
            lines[2 * s].append(jnp.where(low, even, pltpu.roll(odd, HALF, 1)))
            lines[2 * s + 1].append(jnp.where(low, pltpu.roll(even, HALF, 1), odd))
    return jnp.concatenate([jnp.concatenate(line, axis=1) for line in lines], axis=0)


def scatter_lines(out_ref, lines, planes, first, stride):
    rows = out_ref.shape[0] // (stride * planes)
    low = iota((planes, 2 * HALF), 1) < HALF
    for j in range(rows // 2):
        for s in range(2):
            one = lines[2 * s * planes : (2 * s + 1) * planes, j * 128 : (j + 1) * 128]
            two = lines[(2 * s + 1) * planes : (2 * s + 2) * planes, j * 128 : (j + 1) * 128]
            out_ref[pl.ds(2 * j * stride * planes + first + s, planes, stride=stride), :] = jnp.where(
                low, one, pltpu.roll(two, HALF, 1)
            )
            out_ref[pl.ds((2 * j + 1) * stride * planes + first + s, planes, stride=stride), :] = jnp.where(
                low, pltpu.roll(one, HALF, 1), two
            )


def plane_mix(z_inverse, lines):
    planes = z_inverse.shape[0]
    copies = lines.shape[0] // planes
    tiled = jnp.concatenate([jnp.concatenate([z_inverse] * copies, axis=1)] * copies, axis=0)
    same = iota(tiled.shape, 0) // planes == iota(tiled.shape, 1) // planes
    return jnp.dot(
        jnp.where(same, tiled, 0.0), lines, precision=lax.Precision.HIGHEST, preferred_element_type=jnp.float32
    )


def bound(old, seeds, irreversible):
    return jnp.where(seeds == 1, 1.0, jnp.where(irreversible == 1, old, 0.0))


def clamp(damage, update, lower_bound):
    return jnp.minimum(jnp.maximum(damage + update, lower_bound), 1.0)


def first_kernel(
    energy_hbm, old_hbm, seeds_hbm, irreversible_hbm, inverses_hbm,
    out_ref,
    energy_ref, old_ref, seeds_ref, irreversible_ref, inverses_ref, sems,
):
    pairs = [
        (old_hbm, old_ref), (seeds_hbm, seeds_ref), (energy_hbm, energy_ref),
        (inverses_hbm, inverses_ref), (irreversible_hbm, irreversible_ref),
    ]
    copies = [pltpu.make_async_copy(src, dst, sems.at[i]) for i, (src, dst) in enumerate(pairs)]
    for copy in copies:
        copy.start()
    copies[0].wait()
    copies[1].wait()
    damage = jnp.where(seeds_ref[0] == 1, 1.0, old_ref[0])
    send_rows(out_ref, damage, 4, 10)
    copies[2].wait()
    energy = energy_ref[0]
    send_rows(out_ref, energy, 8, 10)
    partial_value = energy - (1.0 + energy) * damage + KAPPA * lane_lap(damage)
    copies[3].wait()
    count = damage.shape[0]
    solved = line_solve(jnp.concatenate([partial_value, damage], axis=0), inverses_ref)
    send_rows(out_ref, solved[:count], 0, 10)
    send_rows(out_ref, solved[count:], 2, 10)
    copies[4].wait()
    send_rows(out_ref, bound(old_ref[0], seeds_ref[0], irreversible_ref[0]), 6, 10)


def cross_kernel(in_ref, inverses_ref, z_ref, out_ref, change_ref):
    z_inverse = z_ref[...]
    planes = z_inverse.shape[0]
    solved_damage = gather_lines(in_ref, planes, 2, 10)
    turned = gather_lines(in_ref, planes, 0, 10) + KAPPA * (
        lane_lap(solved_damage) + plane_lap(solved_damage, planes)
    )
    update = STEP * plane_mix(z_inverse, line_solve(turned, inverses_ref))
    damage = gather_lines(in_ref, planes, 4, 10)
    renewed = clamp(damage, update, gather_lines(in_ref, planes, 6, 10))
    change_ref[...] = jnp.full(change_ref.shape, jnp.sum((renewed - damage) ** 2), jnp.float32)
    scatter_lines(out_ref, renewed, planes, 4, 6)
    energy = gather_lines(in_ref, planes, 8, 10)
    partial_value = energy - (1.0 + energy) * renewed + KAPPA * (lane_lap(renewed) + plane_lap(renewed, planes))
    count = renewed.shape[0]
    solved = line_solve(jnp.concatenate([partial_value, renewed], axis=0), inverses_ref)
    scatter_lines(out_ref, plane_mix(z_inverse, solved[:count]), planes, 0, 6)
    scatter_lines(out_ref, plane_mix(z_inverse, solved[count:]), planes, 2, 6)


def last_kernel(
    in_ref, old_ref, seeds_ref, irreversible_ref, inverses_ref, first_change_ref, damage_ref, change_ref
):
    solved_part = receive_rows(in_ref, 0, 6)
    solved_damage = receive_rows(in_ref, 2, 6)
    update = STEP * line_solve(solved_part + KAPPA * lane_lap(solved_damage), inverses_ref)
    damage = receive_rows(in_ref, 4, 6)
    renewed = clamp(damage, update, bound(old_ref[0], seeds_ref[0], irreversible_ref[0]))
    damage_ref[0] = renewed
    change = jnp.sum((renewed - damage) ** 2)
    lane = iota(change_ref.shape, 1)
    change_ref[...] = jnp.where(lane == 0, first_change_ref[...], jnp.where(lane == 1, change, 0.0))


def call(kernel, outs, *args, direct=True, scratch=()):
    space = pltpu.VMEM if direct else pl.ANY
    if not direct:
        args = [pltpu.with_memory_space_constraint(arg, pltpu.HBM) for arg in args]
    return pl.pallas_call(
        kernel,
        out_shape=[jax.ShapeDtypeStruct(shape, jnp.float32) for shape in outs],
        in_specs=[pl.BlockSpec(memory_space=space) for _ in args],
        out_specs=[pl.BlockSpec(memory_space=pltpu.VMEM) for _ in outs],
        scratch_shapes=scratch,
        compiler_params=pltpu.CompilerParams(vmem_limit_bytes=20 * 1024 * 1024),
    )(*args)


def exchange(rows, axes):
    return lax.all_to_all(rows, axes, split_axis=0, concat_axis=0, tiled=True)


def cross(rows):
    pairs = rows.reshape(-1, 2, 128)
    return exchange(pairs, ALL).reshape(rows.shape)


def local(energy, damage_old, crack_seeds, irreversible, line_inverses, z_inverse):
    planes, rows_here, line_length = energy.shape
    cell_count = planes * rows_here * line_length * lax.axis_size(ALL)
    one = planes * rows_here * line_length // 128
    inputs = (energy, damage_old, crack_seeds, irreversible, line_inverses)
    scratch = [pltpu.VMEM(part.shape, part.dtype) for part in inputs] + [pltpu.SemaphoreType.DMA((5,))]
    (sent,) = call(first_kernel, [(5 * one, 128)], *inputs, direct=False, scratch=scratch)
    sent, change = call(cross_kernel, [(3 * one, 128), (1, 128)], cross(sent), line_inverses, z_inverse)
    damage, change = call(
        last_kernel,
        [energy.shape, (lax.axis_size(PLANE), 128)],
        cross(sent),
        damage_old,
        crack_seeds,
        irreversible,
        line_inverses,
        change,
    )
    plane_sums = jnp.sum(exchange(change, PLANE), axis=0, keepdims=True)
    every = exchange(jnp.broadcast_to(plane_sums, (lax.axis_size(ROW[0]), 128)), ROW[:1])
    global_sums = jnp.sum(every, axis=0)[:ITERS]
    update_norms = jnp.sqrt(global_sums / cell_count + EPSILON) / STEP
    return (damage, update_norms)


def solution(mesh):
    finer = Mesh(mesh.devices.reshape(8, 2, 2, 4, 4), ALL)
    spec = P(COL, ROW, None)
    in_specs = (spec, spec, spec, spec, P(), P())
    return jax.shard_map(local, mesh=finer, in_specs=in_specs, out_specs=(spec, P()), check_vma=False)
```

time: 206 us -> 182 us (0.88)
  blocking collectives: 186 us -> 165 us
  local copies, waits for them, and re-layouts: 3.43 us -> 0.04 us
    all_to_all x5 -> x4, blocking collectives: 186 us -> 165 us  [exchange(): return lax.all_to_all(rows, axes, split_axis=0, concat_axis=0, tiled=True)]
    unnamed x18 -> x10, local copies, waits for them, and re-layouts: 3.3 us -> 0.03 us
    pallas_call x5 -> x3, Pallas kernels: 14.7 us -> 15.9 us  [call(): pl.pallas_call(kernel, out_shape=[jax.ShapeDtypeStruct(shape, jnp.float32...]
where the time goes in v1:
time: 182 us
  blocking collectives  165 us (91%)
  Pallas kernels  15.9 us (9%)
    all_to_all x4, blocking collectives, exchange(): return lax.all_to_all(rows, axes, split_axis=0, concat_axis=0, tiled=True)  165 us
    pallas_call x3, Pallas kernels, call(): pl.pallas_call(kernel, out_shape=[jax.ShapeDtypeStruct(shape, jnp.float32...  15.9 us

profile of v1, /device:TPU:1, one launch (start us, length us, event | category | flops | bytes accessed | tf_op | source)
XLA Modules:
  0.0 181.9 jit_solution(10332196589374956318)
XLA Ops:
  0.6 5.2 %shard_map.77 = f32[5120,128]{1,0:T(8,128)S(1)} custom-call(f32[1,64,2048]{2,1,0:T(8,128)} %energy_hbm.1, f32[1,64,2048]{2,1,0:T(8,128)} %old_ref.1, s32[1,64,2048]{2,1,0:T(8,128)} %seeds_ref.1, s32[1,64,2048]{2,1,0:T(8,128)} %irreversible_ref.1, f32[8,256,256]{2,1,0:T(8,128)} %inverses_ref.3), custom_call_target="tpu_custom_call" | custom-call | tf_op jit(solution)/shard_map/pallas_call | solution.py:221
  5.8 0.0 copy-start
  5.8 0.0 copy-start.4
  5.8 89.7 %all_to_all.25 = f32[2560,2,128]{2,1,0:T(2,128)S(1)} all-to-all(f32[2560,2,128]{2,1,0:T(2,128)S(1)} %bitcast.9), channel_id=1, replica_groups=mesh['row_0'=8,'row_1'=2,'row_2'=2,'col_0'=4,'col_1'=4] {'row_0','row_1'..., dimensions={0} | all-to-all | bytes 5242880 | tf_op jit(solution)/shard_map/all_to_all | solution.py:232
  95.5 0.0 copy-done
  95.5 0.0 copy-done.4
  95.5 7.1 %shard_map.78 = (f32[3072,128]{1,0:T(8,128)S(1)}, f32[1,128]{1,0:T(1,128)S(1)}) custom-call(f32[5120,128]{1,0:T(8,128)S(1)} %bitcast.8, f32[8,256,256]{2,1,0:T(8,128)S(1)} %copy-done, f32[16,16]{1,0:T(8,128)S(1)} %copy-done.4), custom_call_target="tpu_custom_call" | custom-call | tf_op jit(solution)/shard_map/pallas_call | solution.py:221
  102.6 0.0 copy-start.1
  102.6 0.0 copy-start.2
  102.7 0.0 copy-start.3
  102.7 52.5 %all_to_all.26 = f32[1536,2,128]{2,1,0:T(2,128)S(1)} all-to-all(f32[1536,2,128]{2,1,0:T(2,128)S(1)} %bitcast.11), channel_id=1, replica_groups=mesh['row_0'=8,'row_1'=2,'row_2'=2,'col_0'=4,'col_1'=4] {'row_0','row_1'..., dimensions={0} | all-to-all | bytes 3145728 | tf_op jit(solution)/shard_map/all_to_all | solution.py:232
  155.2 0.0 copy-done.1
  155.2 0.0 copy-done.2
  155.2 0.0 copy-done.3
  155.2 3.6 %shard_map.79 = (f32[1,64,2048]{2,1,0:T(8,128)}, f32[64,128]{1,0:T(8,128)S(1)}) custom-call(f32[3072,128]{1,0:T(8,128)S(1)} %bitcast.10, f32[1,64,2048]{2,1,0:T(8,128)S(1)} %copy-done.1, s32[1,64,2048]{2,1,0:T(8,128)S(1)} %copy-done.2, s32[1,64,2048]{2,1,0:T(8,128)S(1)} %copy-done.3, f32[8,256,256]{2,1,0:T(8,128)S(1)} %copy-done, ...), custom_call_target="tpu_custom_call" | custom-call | tf_op jit(solution)/shard_map/pallas_call | solution.py:221
  158.8 12.9 %all_to_all.27 = f32[64,1,128]{2,1,0:T(1,128)S(1)} all-to-all(f32[64,1,128]{2,1,0:T(1,128)S(1)} %bitcast.12), channel_id=1, replica_groups=mesh['row_0'=8,'row_1'=2,'row_2'=2,'col_0'=4,'col_1'=4] {'row_1','row_2'..., dimensions={0} | all-to-all | bytes 65536 | tf_op jit(solution)/shard_map/all_to_all | solution.py:232
  171.8 0.1 reduce_sum.18
  171.8 9.5 %all_to_all.28 = f32[8,1,128]{2,1,0:T(1,128)S(1)} all-to-all(f32[8,1,128]{2,1,0:T(1,128)S(1)} %broadcast_in_dim.2), channel_id=1, replica_groups=mesh['row_0'=8,'row_1'=2,'row_2'=2,'col_0'=4,'col_1'=4] {'row_0'}, dimensions={0} | all-to-all | bytes 8192 | tf_op jit(solution)/shard_map/all_to_all | solution.py:232
  181.4 0.5 sqrt_multiply_fusion
  (2 shorter events, 0.0 us)
Async XLA Ops:
  5.8 89.7 %copy-start = (f32[8,256,256]{2,1,0:T(8,128)S(1)}, f32[8,256,256]{2,1,0:T(8,128)}, u32[]{:S(2)}) copy-start(f32[8,256,256]{2,1,0:T(8,128)} %inverses_ref.3) | copy-start | bytes 6291460
  5.8 89.7 %copy-start.4 = (f32[16,16]{1,0:T(8,128)S(1)}, f32[16,16]{1,0:T(8,128)}, u32[]{:S(2)}) copy-start(f32[16,16]{1,0:T(8,128)} %z_ref.1) | copy-start | bytes 3076
  102.6 52.6 %copy-start.1 = (f32[1,64,2048]{2,1,0:T(8,128)S(1)}, f32[1,64,2048]{2,1,0:T(8,128)}, u32[]{:S(2)}) copy-start(f32[1,64,2048]{2,1,0:T(8,128)} %old_ref.1) | copy-start | bytes 1572868
  102.6 52.6 %copy-start.2 = (s32[1,64,2048]{2,1,0:T(8,128)S(1)}, s32[1,64,2048]{2,1,0:T(8,128)}, u32[]{:S(2)}) copy-start(s32[1,64,2048]{2,1,0:T(8,128)} %seeds_ref.1) | copy-start | bytes 1572868
  102.7 52.6 %copy-start.3 = (s32[1,64,2048]{2,1,0:T(8,128)S(1)}, s32[1,64,2048]{2,1,0:T(8,128)}, u32[]{:S(2)}) copy-start(s32[1,64,2048]{2,1,0:T(8,128)} %irreversible_ref.1) | copy-start | bytes 1572868

commit v2 on v1

--- a/solution.py
+++ b/solution.py
@@ -40,27 +40,47 @@
     return (ahead - field) + (behind - field)
 
 
-def line_solve(lines, inverses_ref):
-    count = lines.shape[0]
+def halves(value):
+    high = value.astype(jnp.bfloat16)
+    return high, (value - high.astype(jnp.float32)).astype(jnp.bfloat16)
+
+
+def product(rows, high, low, dims):
+    count = rows.shape[0]
+    rows_high, rows_low = halves(rows)
+    both = lax.dot_general(
+        jnp.concatenate([rows_high, rows_low], axis=0), high, (dims, ((), ())), preferred_element_type=jnp.float32
+    )
+    rest = lax.dot_general(rows_high, low, (dims, ((), ())), preferred_element_type=jnp.float32)
+    return both[:count] + both[count:] + rest
+
+
+def split_inverses(inverses_ref, high_ref, low_ref, ends_ref):
     blocks, cells, _ = inverses_ref.shape
-    unit_row = iota((8, cells), 0)
-    unit_lane = iota((8, cells), 1)
+    unit_row = iota((16, cells), 0)
+    unit_lane = iota((16, cells), 1)
     units = jnp.where(
         ((unit_row == 0) & (unit_lane == 0)) | ((unit_row == 1) & (unit_lane == cells - 1)), 1.0, 0.0
-    )
+    ).astype(jnp.bfloat16)
+    for k in range(blocks):
+        high, low = halves(inverses_ref[k])
+        high_ref[k] = high
+        low_ref[k] = low
+        dims = (((1,), (1,)), ((), ()))
+        ends = lax.dot_general(units, high, dims, preferred_element_type=jnp.float32) + lax.dot_general(
+            units, low, dims, preferred_element_type=jnp.float32
+        )
+        ends_ref[k] = ends[:8]
+
+
+def line_solve(lines, high_ref, low_ref, ends_ref):
+    count = lines.shape[0]
+    blocks, cells, _ = high_ref.shape
     products, firsts, lasts = [], [], []
     for k in range(blocks):
-        stacked = jnp.concatenate([lines[:, k * cells : (k + 1) * cells], units], axis=0)
-        result = lax.dot_general(
-            stacked,
-            inverses_ref[k],
-            (((1,), (1,)), ((), ())),
-            precision=lax.Precision.HIGHEST,
-            preferred_element_type=jnp.float32,
-        )
-        products.append(result[:count])
-        firsts.append(result[count : count + 1])
-        lasts.append(result[count + 1 : count + 2])
+        products.append(product(lines[:, k * cells : (k + 1) * cells], high_ref[k], low_ref[k], ((1,), (1,))))
+        firsts.append(ends_ref[k, 0:1, :])
+        lasts.append(ends_ref[k, 1:2, :])
     inflow = [jnp.zeros((count, 1), jnp.float32)]
     heads = []
     for k in range(blocks):
@@ -138,9 +158,8 @@
     copies = lines.shape[0] // planes
     tiled = jnp.concatenate([jnp.concatenate([z_inverse] * copies, axis=1)] * copies, axis=0)
     same = iota(tiled.shape, 0) // planes == iota(tiled.shape, 1) // planes
-    return jnp.dot(
-        jnp.where(same, tiled, 0.0), lines, precision=lax.Precision.HIGHEST, preferred_element_type=jnp.float32
-    )
+    high, low = halves(lines)
+    return product(jnp.where(same, tiled, 0.0), high, low, ((1,), (0,)))
 
 
 def bound(old, seeds, irreversible):
@@ -153,7 +172,7 @@
 
 def first_kernel(
     energy_hbm, old_hbm, seeds_hbm, irreversible_hbm, inverses_hbm,
-    out_ref,
+    out_ref, high_ref, low_ref, ends_ref,
     energy_ref, old_ref, seeds_ref, irreversible_ref, inverses_ref, sems,
 ):
     pairs = [
@@ -172,22 +191,23 @@
     send_rows(out_ref, energy, 8, 10)
     partial_value = energy - (1.0 + energy) * damage + KAPPA * lane_lap(damage)
     copies[3].wait()
+    split_inverses(inverses_ref, high_ref, low_ref, ends_ref)
     count = damage.shape[0]
-    solved = line_solve(jnp.concatenate([partial_value, damage], axis=0), inverses_ref)
+    solved = line_solve(jnp.concatenate([partial_value, damage], axis=0), high_ref, low_ref, ends_ref)
     send_rows(out_ref, solved[:count], 0, 10)
     send_rows(out_ref, solved[count:], 2, 10)
     copies[4].wait()
     send_rows(out_ref, bound(old_ref[0], seeds_ref[0], irreversible_ref[0]), 6, 10)
 
 
-def cross_kernel(in_ref, inverses_ref, z_ref, out_ref, change_ref):
+def cross_kernel(in_ref, high_ref, low_ref, ends_ref, z_ref, out_ref, change_ref):
     z_inverse = z_ref[...]
     planes = z_inverse.shape[0]
     solved_damage = gather_lines(in_ref, planes, 2, 10)
     turned = gather_lines(in_ref, planes, 0, 10) + KAPPA * (
         lane_lap(solved_damage) + plane_lap(solved_damage, planes)
     )
-    update = STEP * plane_mix(z_inverse, line_solve(turned, inverses_ref))
+    update = STEP * plane_mix(z_inverse, line_solve(turned, high_ref, low_ref, ends_ref))
     damage = gather_lines(in_ref, planes, 4, 10)
     renewed = clamp(damage, update, gather_lines(in_ref, planes, 6, 10))
     change_ref[...] = jnp.full(change_ref.shape, jnp.sum((renewed - damage) ** 2), jnp.float32)
@@ -195,17 +215,18 @@
     energy = gather_lines(in_ref, planes, 8, 10)
     partial_value = energy - (1.0 + energy) * renewed + KAPPA * (lane_lap(renewed) + plane_lap(renewed, planes))
     count = renewed.shape[0]
-    solved = line_solve(jnp.concatenate([partial_value, renewed], axis=0), inverses_ref)
+    solved = line_solve(jnp.concatenate([partial_value, renewed], axis=0), high_ref, low_ref, ends_ref)
     scatter_lines(out_ref, plane_mix(z_inverse, solved[:count]), planes, 0, 6)
     scatter_lines(out_ref, plane_mix(z_inverse, solved[count:]), planes, 2, 6)
 
 
 def last_kernel(
-    in_ref, old_ref, seeds_ref, irreversible_ref, inverses_ref, first_change_ref, damage_ref, change_ref
+    in_ref, old_ref, seeds_ref, irreversible_ref, high_ref, low_ref, ends_ref, first_change_ref, damage_ref, change_ref
 ):
     solved_part = receive_rows(in_ref, 0, 6)
     solved_damage = receive_rows(in_ref, 2, 6)
-    update = STEP * line_solve(solved_part + KAPPA * lane_lap(solved_damage), inverses_ref)
+    turned = solved_part + KAPPA * lane_lap(solved_damage)
+    update = STEP * line_solve(turned, high_ref, low_ref, ends_ref)
     damage = receive_rows(in_ref, 4, 6)
     renewed = clamp(damage, update, bound(old_ref[0], seeds_ref[0], irreversible_ref[0]))
     damage_ref[0] = renewed
@@ -220,7 +241,7 @@
         args = [pltpu.with_memory_space_constraint(arg, pltpu.HBM) for arg in args]
     return pl.pallas_call(
         kernel,
-        out_shape=[jax.ShapeDtypeStruct(shape, jnp.float32) for shape in outs],
+        out_shape=[jax.ShapeDtypeStruct(shape, dtype) for shape, dtype in outs],
         in_specs=[pl.BlockSpec(memory_space=space) for _ in args],
         out_specs=[pl.BlockSpec(memory_space=pltpu.VMEM) for _ in outs],
         scratch_shapes=scratch,
@@ -243,16 +264,26 @@
     one = planes * rows_here * line_length // 128
     inputs = (energy, damage_old, crack_seeds, irreversible, line_inverses)
     scratch = [pltpu.VMEM(part.shape, part.dtype) for part in inputs] + [pltpu.SemaphoreType.DMA((5,))]
-    (sent,) = call(first_kernel, [(5 * one, 128)], *inputs, direct=False, scratch=scratch)
-    sent, change = call(cross_kernel, [(3 * one, 128), (1, 128)], cross(sent), line_inverses, z_inverse)
+    f32, bf16 = jnp.float32, jnp.bfloat16
+    blocks, cells, _ = line_inverses.shape
+    sent, *split = call(
+        first_kernel,
+        [((5 * one, 128), f32), (line_inverses.shape, bf16), (line_inverses.shape, bf16), ((blocks, 8, cells), f32)],
+        *inputs,
+        direct=False,
+        scratch=scratch,
+    )
+    sent, change = call(
+        cross_kernel, [((3 * one, 128), f32), ((1, 128), f32)], cross(sent), *split, z_inverse
+    )
     damage, change = call(
         last_kernel,
-        [energy.shape, (lax.axis_size(PLANE), 128)],
+        [(energy.shape, f32), ((lax.axis_size(PLANE), 128), f32)],
         cross(sent),
         damage_old,
         crack_seeds,
         irreversible,
-        line_inverses,
+        *split,
         change,
     )
     plane_sums = jnp.sum(exchange(change, PLANE), axis=0, keepdims=True)

time: 182 us -> 177 us (0.973)
  Pallas kernels: 15.9 us -> 10.4 us
    pallas_call x3, Pallas kernels: 15.9 us -> 10.4 us  [call(): pl.pallas_call(kernel, out_shape=[jax.ShapeDtypeStruct(shape, dtype) for...]
where the time goes in v2:
time: 177 us; the launch traced here: 176 us
  blocking collectives  165 us (93%)
  Pallas kernels  10.4 us (6%)
    all_to_all x4, blocking collectives, exchange(): return lax.all_to_all(rows, axes, split_axis=0, concat_axis=0, tiled=True)  165 us
    pallas_call x3, Pallas kernels, call(): pl.pallas_call(kernel, out_shape=[jax.ShapeDtypeStruct(shape, dtype) for...  10.4 us

profile of v2, /device:TPU:1, one launch (start us, length us, event | category | flops | bytes accessed | tf_op | source)
XLA Modules:
  0.0 176.4 jit_solution(14717205993151956999)
XLA Ops:
  0.6 4.3 %shard_map.77 = (f32[5120,128]{1,0:T(8,128)S(1)}, bf16[8,256,256]{2,1,0:T(8,128)(2,1)S(1)}, bf16[8,256,256]{2,1,0:T(8,128)(2,1)S(1)}, f32[8,8,256]{2,1,0:T(8,128)S(1)}) custom-call(f32[1,64,2048]{2,1,0:T(8,128)} %energy_hbm.1, f32[1,64,2048]{2,1,0:T(8,128)} %old_ref.1, s32[1,64,2048]{2,1,0:T(8,128)} %seeds_ref.1, s32[1,64,2048]{2,1,0:T(8,128)} %irreversible_ref.1, ...), custom_call_target="tpu_custom_call" | custom-call | tf_op jit(solution)/shard_map/pallas_call | solution.py:242
  4.9 0.0 copy-start.3
  4.9 89.7 %all_to_all.25 = f32[2560,2,128]{2,1,0:T(2,128)S(1)} all-to-all(f32[2560,2,128]{2,1,0:T(2,128)S(1)} %bitcast.10), channel_id=1, replica_groups=mesh['row_0'=8,'row_1'=2,'row_2'=2,'col_0'=4,'col_1'=4] {'row_0','row_1'..., dimensions={0} | all-to-all | bytes 5242880 | tf_op jit(solution)/shard_map/all_to_all | solution.py:253
  94.6 0.0 copy-done.3
  94.6 3.8 %shard_map.78 = (f32[3072,128]{1,0:T(8,128)S(1)}, f32[1,128]{1,0:T(1,128)S(1)}) custom-call(f32[5120,128]{1,0:T(8,128)S(1)} %bitcast.8, bf16[8,256,256]{2,1,0:T(8,128)(2,1)S(1)} %get-tuple-element.11.high_ref, bf16[8,256,256]{2,1,0:T(8,128)(2,1)S(1)} %get-tuple-element.12.low_ref, f32[8,8,256]{2,1,0:T(8,128)S(1)} %get-tuple-element.13.ends_ref, ...), custom_call_target="tpu_custom_call" | custom-call | tf_op jit(solution)/shard_map/pallas_call | solution.py:242
  98.4 0.0 copy-start
  98.4 0.0 copy-start.1
  98.4 0.0 copy-start.2
  98.5 52.6 %all_to_all.26 = f32[1536,2,128]{2,1,0:T(2,128)S(1)} all-to-all(f32[1536,2,128]{2,1,0:T(2,128)S(1)} %bitcast.11), channel_id=1, replica_groups=mesh['row_0'=8,'row_1'=2,'row_2'=2,'col_0'=4,'col_1'=4] {'row_0','row_1'..., dimensions={0} | all-to-all | bytes 3145728 | tf_op jit(solution)/shard_map/all_to_all | solution.py:253
  151.0 0.0 copy-done
  151.0 0.0 copy-done.1
  151.0 0.0 copy-done.2
  151.0 2.3 %shard_map.79 = (f32[1,64,2048]{2,1,0:T(8,128)}, f32[64,128]{1,0:T(8,128)S(1)}) custom-call(f32[3072,128]{1,0:T(8,128)S(1)} %bitcast.9, f32[1,64,2048]{2,1,0:T(8,128)S(1)} %copy-done, s32[1,64,2048]{2,1,0:T(8,128)S(1)} %copy-done.1, s32[1,64,2048]{2,1,0:T(8,128)S(1)} %copy-done.2, bf16[8,256,256]{2,1,0:T(8,128)(2,1)S(1)} %get-tuple-element.11.high_ref, ...), custom_call_target="tpu_custom_call" | custom-call | tf_op jit(solution)/shard_map/pallas_call | solution.py:242
  153.3 12.9 %all_to_all.27 = f32[64,1,128]{2,1,0:T(1,128)S(1)} all-to-all(f32[64,1,128]{2,1,0:T(1,128)S(1)} %bitcast.12), channel_id=1, replica_groups=mesh['row_0'=8,'row_1'=2,'row_2'=2,'col_0'=4,'col_1'=4] {'row_1','row_2'..., dimensions={0} | all-to-all | bytes 65536 | tf_op jit(solution)/shard_map/all_to_all | solution.py:253
  166.2 0.1 reduce_sum.18
  166.3 9.5 %all_to_all.28 = f32[8,1,128]{2,1,0:T(1,128)S(1)} all-to-all(f32[8,1,128]{2,1,0:T(1,128)S(1)} %broadcast_in_dim.2), channel_id=1, replica_groups=mesh['row_0'=8,'row_1'=2,'row_2'=2,'col_0'=4,'col_1'=4] {'row_0'}, dimensions={0} | all-to-all | bytes 8192 | tf_op jit(solution)/shard_map/all_to_all | solution.py:253
  175.9 0.5 sqrt_multiply_fusion
  (2 shorter events, 0.0 us)
Async XLA Ops:
  4.9 89.7 %copy-start.3 = (f32[16,16]{1,0:T(8,128)S(1)}, f32[16,16]{1,0:T(8,128)}, u32[]{:S(2)}) copy-start(f32[16,16]{1,0:T(8,128)} %z_ref.1) | copy-start | bytes 3076
  98.4 52.6 %copy-start = (f32[1,64,2048]{2,1,0:T(8,128)S(1)}, f32[1,64,2048]{2,1,0:T(8,128)}, u32[]{:S(2)}) copy-start(f32[1,64,2048]{2,1,0:T(8,128)} %old_ref.1) | copy-start | bytes 1572868
  98.4 52.6 %copy-start.1 = (s32[1,64,2048]{2,1,0:T(8,128)S(1)}, s32[1,64,2048]{2,1,0:T(8,128)}, u32[]{:S(2)}) copy-start(s32[1,64,2048]{2,1,0:T(8,128)} %seeds_ref.1) | copy-start | bytes 1572868
  98.4 52.6 %copy-start.2 = (s32[1,64,2048]{2,1,0:T(8,128)S(1)}, s32[1,64,2048]{2,1,0:T(8,128)}, u32[]{:S(2)}) copy-start(s32[1,64,2048]{2,1,0:T(8,128)} %irreversible_ref.1) | copy-start | bytes 1572868

commit v3 on v2

v3 whole, which is shorter than its diff:
```python
import jax
import jax.numpy as jnp
from jax import lax
from jax.experimental import pallas as pl
from jax.experimental.pallas import tpu as pltpu
from jax.sharding import Mesh
from jax.sharding import PartitionSpec as P

ROW = ("row_0", "row_1", "row_2")
COL = ("col_0", "col_1")
ALL = ROW + COL
PLANE = ROW[1:] + COL

ITERS = 2

KAPPA = 2.0
STEP = 0.02
COUPLE = 0.5
EPSILON = 1e-06
HALF = 64


def iota(shape, axis):
    return lax.broadcasted_iota(jnp.int32, shape, axis)


def lane_lap(field):
    extent = field.shape[1]
    lane = iota(field.shape, 1)
    ahead = jnp.where(lane == extent - 1, field, pltpu.roll(field, extent - 1, 1))
    behind = jnp.where(lane == 0, field, pltpu.roll(field, 1, 1))
    return (ahead - field) + (behind - field)


def plane_lap(field, planes):
    extent = field.shape[0]
    plane = iota(field.shape, 0) % planes
    ahead = jnp.where(plane == planes - 1, field, pltpu.roll(field, extent - 1, 0))
    behind = jnp.where(plane == 0, field, pltpu.roll(field, 1, 0))
    return (ahead - field) + (behind - field)


def halves(value):
    high = value.astype(jnp.bfloat16)
    return high, (value - high.astype(jnp.float32)).astype(jnp.bfloat16)


def product(rows, high, low, dims):
    count = rows.shape[0]
    rows_high, rows_low = halves(rows)
    both = lax.dot_general(
        jnp.concatenate([rows_high, rows_low], axis=0), high, (dims, ((), ())), preferred_element_type=jnp.float32
    )
    rest = lax.dot_general(rows_high, low, (dims, ((), ())), preferred_element_type=jnp.float32)
    return both[:count] + both[count:] + rest


def split_inverses(inverses_ref, high_ref, low_ref, ends_ref):
    blocks, cells, _ = inverses_ref.shape
    unit_row = iota((16, cells), 0)
    unit_lane = iota((16, cells), 1)
    units = jnp.where(
        ((unit_row == 0) & (unit_lane == 0)) | ((unit_row == 1) & (unit_lane == cells - 1)), 1.0, 0.0
    ).astype(jnp.bfloat16)
    for k in range(blocks):
        high, low = halves(inverses_ref[k])
        high_ref[k] = high
        low_ref[k] = low
        dims = (((1,), (1,)), ((), ()))
        ends = lax.dot_general(units, high, dims, preferred_element_type=jnp.float32) + lax.dot_general(
            units, low, dims, preferred_element_type=jnp.float32
        )
        ends_ref[k] = ends[:8]
        ends_ref[k, 2:3, :] = jnp.broadcast_to(ends[0:1, 0:1], (1, cells))
        ends_ref[k, 3:4, :] = jnp.broadcast_to(ends[0:1, cells - 1 : cells], (1, cells))
        ends_ref[k, 4:5, :] = jnp.broadcast_to(ends[1:2, 0:1], (1, cells))


def line_solve(lines, high_ref, low_ref, ends_ref):
    count = lines.shape[0]
    blocks, cells, _ = high_ref.shape
    products, firsts, lasts = [], [], []
    for k in range(blocks):
        products.append(product(lines[:, k * cells : (k + 1) * cells], high_ref[k], low_ref[k], ((1,), (1,))))
        firsts.append(ends_ref[k, 0:1, :])
        lasts.append(ends_ref[k, 1:2, :])
    wide = (count, 128)
    inflow, outflow = [None], [None] * blocks
    heads = [jnp.broadcast_to(products[0][:, 0:1], wide)]
    carried = jnp.broadcast_to(products[0][:, cells - 1 : cells], wide)
    for k in range(1, blocks):
        inflow.append(COUPLE * carried)
        heads.append(jnp.broadcast_to(products[k][:, 0:1], wide) + inflow[k] * ends_ref[k, 2:3, :128])
        if k < blocks - 1:
            carried = (
                jnp.broadcast_to(products[k][:, cells - 1 : cells], wide) + inflow[k] * ends_ref[k, 3:4, :128]
            )
    carried = heads[blocks - 1]
    for k in range(blocks - 2, -1, -1):
        outflow[k] = COUPLE * carried
        carried = heads[k] + outflow[k] * ends_ref[k, 4:5, :128]
    solved = []
    for k in range(blocks):
        for half in range(0, cells, 128):
            value = products[k][:, half : half + 128]
            if k > 0:
                value = value + inflow[k] * firsts[k][:, half : half + 128]
            if k < blocks - 1:
                value = value + outflow[k] * lasts[k][:, half : half + 128]
            solved.append(value)
    return jnp.concatenate(solved, axis=1)


def low_half(count):
    return iota((count, 2 * HALF), 1) < HALF


def send_pair(out_ref, flat_ref, stacked, first, stride):
    chunks = out_ref.shape[0] // stride
    for t in range(0, 4 * chunks, 128):
        flat_ref[t : t + 128, :] = stacked[:, t : t + 128].T
    for i in range(4):
        out_ref[pl.ds(first + i, chunks, stride=stride), :] = flat_ref[pl.ds(i, chunks, stride=4), :]


def send_single(out_ref, flat_ref, field, first, stride):
    chunks = out_ref.shape[0] // stride
    doubled = jnp.concatenate([field, field], axis=0)
    for t in range(0, 4 * chunks, 128):
        flat_ref[t : t + 128, :] = doubled[:, t : t + 128].T
    for i in range(2):
        out_ref[pl.ds(first + i, chunks, stride=stride), :] = jnp.where(
            low_half(chunks),
            flat_ref[pl.ds(i, chunks, stride=4), :],
            flat_ref[pl.ds(i + 2, chunks, stride=4), :],
        )


def gather_row(in_ref, planes, at, stride):
    rows = in_ref.shape[0] // (stride * planes)
    low = low_half(planes)
    ones, twos = [], []
    for j in range(rows // 2):
        even = in_ref[pl.ds(2 * j * stride * planes + at, planes, stride=stride), :]
        odd = in_ref[pl.ds((2 * j + 1) * stride * planes + at, planes, stride=stride), :]
        ones.append(jnp.where(low, even, pltpu.roll(odd, HALF, 1)))
        twos.append(jnp.where(low, pltpu.roll(even, HALF, 1), odd))
    return jnp.concatenate(ones, axis=1), jnp.concatenate(twos, axis=1)


def scatter_row(out_ref, ones, twos, planes, at, stride):
    rows = out_ref.shape[0] // (stride * planes)
    low = low_half(planes)
    for j in range(rows // 2):
        one = ones[:, j * 128 : (j + 1) * 128]
        two = twos[:, j * 128 : (j + 1) * 128]
        out_ref[pl.ds(2 * j * stride * planes + at, planes, stride=stride), :] = jnp.where(
            low, one, pltpu.roll(two, HALF, 1)
        )
        out_ref[pl.ds((2 * j + 1) * stride * planes + at, planes, stride=stride), :] = jnp.where(
            low, pltpu.roll(one, HALF, 1), two
        )


def gather_pair(in_ref, planes, first, stride):
    pairs = [gather_row(in_ref, planes, first + i, stride) for i in range(4)]
    return [jnp.concatenate(part, axis=0) for part in zip(*pairs)]


def gather_single(in_ref, planes, first, stride):
    pairs = [gather_row(in_ref, planes, first + i, stride) for i in range(2)]
    return jnp.concatenate([part[half] for half in range(2) for part in pairs], axis=0)


def plane_mix(z_inverse, lines):
    planes = z_inverse.shape[0]
    copies = lines.shape[0] // planes
    tiled = jnp.concatenate([jnp.concatenate([z_inverse] * copies, axis=1)] * copies, axis=0)
    same = iota(tiled.shape, 0) // planes == iota(tiled.shape, 1) // planes
    high, low = halves(lines)
    return product(jnp.where(same, tiled, 0.0), high, low, ((1,), (0,)))


def bound(old, seeds, irreversible):
    return jnp.where(seeds == 1, 1.0, jnp.where(irreversible == 1, old, 0.0))


def clamp(damage, update, lower_bound):
    return jnp.minimum(jnp.maximum(damage + update, lower_bound), 1.0)


def first_kernel(
    energy_hbm, old_hbm, seeds_hbm, irreversible_hbm, inverses_hbm,
    out_ref, high_ref, low_ref, ends_ref,
    energy_ref, old_ref, seeds_ref, irreversible_ref, inverses_ref, flat_refs, sems,
):
    pairs = [
        (inverses_hbm, inverses_ref), (old_hbm, old_ref), (seeds_hbm, seeds_ref),
        (energy_hbm, energy_ref), (irreversible_hbm, irreversible_ref),
    ]
    copies = [pltpu.make_async_copy(src, dst, sems.at[i]) for i, (src, dst) in enumerate(pairs)]
    for copy in copies:
        copy.start()
    copies[0].wait()
    split_inverses(inverses_ref, high_ref, low_ref, ends_ref)
    for copy in copies[1:]:
        copy.wait()
    damage = jnp.where(seeds_ref[0] == 1, 1.0, old_ref[0])
    energy = energy_ref[0]
    partial_value = energy - (1.0 + energy) * damage + KAPPA * lane_lap(damage)
    solved = line_solve(jnp.concatenate([partial_value, damage], axis=0), high_ref, low_ref, ends_ref)
    lower = bound(old_ref[0], seeds_ref[0], irreversible_ref[0])
    send_pair(out_ref, flat_refs.at[0], jnp.concatenate([damage, lower], axis=0), 4, 10)
    send_single(out_ref, flat_refs.at[1], energy, 8, 10)
    send_pair(out_ref, flat_refs.at[2], solved, 0, 10)


def cross_kernel(in_ref, high_ref, low_ref, ends_ref, z_ref, out_ref, change_ref):
    z_inverse = z_ref[...]
    planes = z_inverse.shape[0]
    solved_part, solved_damage = gather_pair(in_ref, planes, 0, 10)
    turned = solved_part + KAPPA * (lane_lap(solved_damage) + plane_lap(solved_damage, planes))
    update = STEP * plane_mix(z_inverse, line_solve(turned, high_ref, low_ref, ends_ref))
    damage, lower = gather_pair(in_ref, planes, 4, 10)
    renewed = clamp(damage, update, lower)
    change_ref[...] = jnp.full(change_ref.shape, jnp.sum((renewed - damage) ** 2), jnp.float32)
    energy = gather_single(in_ref, planes, 8, 10)
    partial_value = energy - (1.0 + energy) * renewed + KAPPA * (lane_lap(renewed) + plane_lap(renewed, planes))
    count = renewed.shape[0]
    solved = line_solve(jnp.concatenate([partial_value, renewed], axis=0), high_ref, low_ref, ends_ref)
    solved_part = plane_mix(z_inverse, solved[:count])
    solved_damage = plane_mix(z_inverse, solved[count:])
    steps = KAPPA * (solved_damage[planes:] - solved_damage[:-planes])
    rim = jnp.zeros((planes, solved.shape[1]), jnp.float32)
    solved_part = solved_part + jnp.concatenate([steps, rim], axis=0) - jnp.concatenate([rim, steps], axis=0)
    for i in range(4):
        part = slice(i * planes, (i + 1) * planes)
        scatter_row(out_ref, solved_part[part], renewed[part], planes, i, 5)
    scatter_row(out_ref, solved_damage[:planes], solved_damage[-planes:], planes, 4, 5)


def last_kernel(
    in_ref, old_ref, seeds_ref, irreversible_ref, high_ref, low_ref, ends_ref, first_change_ref,
    damage_ref, change_ref,
    flat_ref,
):
    chunks = in_ref.shape[0] // 5
    edges = in_ref[pl.ds(4, chunks, stride=5), :]
    inner = low_half(chunks) & (iota((chunks, 128), 0) < chunks - 1)
    steps = pltpu.roll(edges, chunks - 1, 0) - pltpu.roll(edges, HALF, 1)
    steps = jnp.where(inner, KAPPA * steps, 0.0)
    for i in range(4):
        value = in_ref[pl.ds(i, chunks, stride=5), :]
        if i == 0:
            value = value - pltpu.roll(steps, 1, 0)
        if i == 3:
            value = value + steps
        flat_ref[pl.ds(i, chunks, stride=4), :] = value
    tiles = [flat_ref[t : t + 128, :].T for t in range(0, 4 * chunks, 128)]
    turned = jnp.concatenate([tile[:HALF] for tile in tiles], axis=1)
    damage = jnp.concatenate([tile[HALF:] for tile in tiles], axis=1)
    update = STEP * line_solve(turned, high_ref, low_ref, ends_ref)
    renewed = clamp(damage, update, bound(old_ref[0], seeds_ref[0], irreversible_ref[0]))
    damage_ref[0] = renewed
    change = jnp.sum((renewed - damage) ** 2)
    lane = iota(change_ref.shape, 1)
    change_ref[...] = jnp.where(lane == 0, first_change_ref[...], jnp.where(lane == 1, change, 0.0))


def call(kernel, outs, *args, direct=True, scratch=()):
    space = pltpu.VMEM if direct else pl.ANY
    if not direct:
        args = [pltpu.with_memory_space_constraint(arg, pltpu.HBM) for arg in args]
    return pl.pallas_call(
        kernel,
        out_shape=[jax.ShapeDtypeStruct(shape, dtype) for shape, dtype in outs],
        in_specs=[pl.BlockSpec(memory_space=space) for _ in args],
        out_specs=[pl.BlockSpec(memory_space=pltpu.VMEM) for _ in outs],
        scratch_shapes=scratch,
        compiler_params=pltpu.CompilerParams(vmem_limit_bytes=20 * 1024 * 1024),
    )(*args)


def exchange(rows, axes):
    return lax.all_to_all(rows, axes, split_axis=0, concat_axis=0, tiled=True)


def cross(rows):
    return exchange(rows.reshape(-1, 1, 128), ALL).reshape(rows.shape)


def local(energy, damage_old, crack_seeds, irreversible, line_inverses, z_inverse):
    planes, rows_here, line_length = energy.shape
    cell_count = planes * rows_here * line_length * lax.axis_size(ALL)
    one = planes * rows_here * line_length // 128
    inputs = (energy, damage_old, crack_seeds, irreversible, line_inverses)
    scratch = [pltpu.VMEM(part.shape, part.dtype) for part in inputs]
    scratch += [pltpu.VMEM((3, 2 * one, 128), jnp.float32), pltpu.SemaphoreType.DMA((5,))]
    f32, bf16 = jnp.float32, jnp.bfloat16
    blocks, cells, _ = line_inverses.shape
    sent, *split = call(
        first_kernel,
        [((5 * one, 128), f32), (line_inverses.shape, bf16), (line_inverses.shape, bf16), ((blocks, 8, cells), f32)],
        *inputs,
        direct=False,
        scratch=scratch,
    )
    sent, change = call(
        cross_kernel, [((5 * one // 2, 128), f32), ((1, 128), f32)], cross(sent), *split, z_inverse
    )
    damage, change = call(
        last_kernel,
        [(energy.shape, f32), ((lax.axis_size(PLANE), 128), f32)],
        cross(sent),
        damage_old,
        crack_seeds,
        irreversible,
        *split,
        change,
        scratch=[pltpu.VMEM((2 * one, 128), f32)],
    )
    plane_sums = jnp.sum(exchange(change, PLANE), axis=0, keepdims=True)
    every = exchange(jnp.broadcast_to(plane_sums, (lax.axis_size(ROW[0]), 128)), ROW[:1])
    global_sums = jnp.sum(every, axis=0)[:ITERS]
    update_norms = jnp.sqrt(global_sums / cell_count + EPSILON) / STEP
    return (damage, update_norms)


def solution(mesh):
    finer = Mesh(mesh.devices.reshape(8, 2, 2, 4, 4), ALL)
    spec = P(COL, ROW, None)
    in_specs = (spec, spec, spec, spec, P(), P())
    return jax.shard_map(local, mesh=finer, in_specs=in_specs, out_specs=(spec, P()), check_vma=False)
```

time: 177 us -> 171 us (0.966)
  blocking collectives: 165 us -> 159 us
    all_to_all x4, blocking collectives: 165 us -> 159 us  [exchange(): return lax.all_to_all(rows, axes, split_axis=0, concat_axis=0, tiled=True)]
where the time goes in v3:
time: 171 us
  blocking collectives  159 us (93%)
  Pallas kernels  10.4 us (6%)
    all_to_all x4, blocking collectives, exchange(): return lax.all_to_all(rows, axes, split_axis=0, concat_axis=0, tiled=True)  159 us
    pallas_call x3, Pallas kernels, call(): pl.pallas_call(kernel, out_shape=[jax.ShapeDtypeStruct(shape, dtype) for...  10.4 us

profile of v3, /device:TPU:1, one launch (start us, length us, event | category | flops | bytes accessed | tf_op | source)
XLA Modules:
  0.0 170.8 jit_solution(4001966848895915584)
XLA Ops:
  0.6 4.7 %shard_map.77 = (f32[5120,128]{1,0:T(8,128)S(1)}, bf16[8,256,256]{2,1,0:T(8,128)(2,1)S(1)}, bf16[8,256,256]{2,1,0:T(8,128)(2,1)S(1)}, f32[8,8,256]{2,1,0:T(8,128)S(1)}) custom-call(f32[1,64,2048]{2,1,0:T(8,128)} %energy_hbm.1, f32[1,64,2048]{2,1,0:T(8,128)} %old_ref.1, s32[1,64,2048]{2,1,0:T(8,128)} %seeds_ref.1, s32[1,64,2048]{2,1,0:T(8,128)} %irreversible_ref.1, ...), custom_call_target="tpu_custom_call" | custom-call | tf_op jit(solution)/shard_map/pallas_call | solution.py:274
  5.3 0.0 copy-start.3
  5.3 89.7 %all_to_all.25 = f32[5120,1,128]{2,1,0:T(1,128)S(1)} all-to-all(f32[5120,1,128]{2,1,0:T(1,128)S(1)} %bitcast.14), channel_id=1, replica_groups=mesh['row_0'=8,'row_1'=2,'row_2'=2,'col_0'=4,'col_1'=4] {'row_0','row_1'..., dimensions={0} | all-to-all | bytes 5242880 | tf_op jit(solution)/shard_map/all_to_all | solution.py:285
  95.0 0.0 copy-done.3
  95.0 3.6 %shard_map.78 = (f32[2560,128]{1,0:T(8,128)S(1)}, f32[1,128]{1,0:T(1,128)S(1)}) custom-call(f32[5120,128]{1,0:T(8,128)S(1)} %bitcast.12, bf16[8,256,256]{2,1,0:T(8,128)(2,1)S(1)} %get-tuple-element.11.high_ref, bf16[8,256,256]{2,1,0:T(8,128)(2,1)S(1)} %get-tuple-element.12.low_ref, f32[8,8,256]{2,1,0:T(8,128)S(1)} %get-tuple-element.13.ends_ref, ...), custom_call_target="tpu_custom_call" | custom-call | tf_op jit(solution)/shard_map/pallas_call | solution.py:274
  98.6 0.0 copy-start
  98.7 0.0 copy-start.1
  98.7 0.0 copy-start.2
  98.7 46.9 %all_to_all.26 = f32[2560,1,128]{2,1,0:T(1,128)S(1)} all-to-all(f32[2560,1,128]{2,1,0:T(1,128)S(1)} %bitcast.15), channel_id=1, replica_groups=mesh['row_0'=8,'row_1'=2,'row_2'=2,'col_0'=4,'col_1'=4] {'row_0','row_1'..., dimensions={0} | all-to-all | bytes 2621440 | tf_op jit(solution)/shard_map/all_to_all | solution.py:285
  145.6 0.0 copy-done
  145.6 0.0 copy-done.1
  145.6 0.0 copy-done.2
  145.6 2.1 %shard_map.79 = (f32[1,64,2048]{2,1,0:T(8,128)}, f32[64,128]{1,0:T(8,128)S(1)}) custom-call(f32[2560,128]{1,0:T(8,128)S(1)} %bitcast.13, f32[1,64,2048]{2,1,0:T(8,128)S(1)} %copy-done, s32[1,64,2048]{2,1,0:T(8,128)S(1)} %copy-done.1, s32[1,64,2048]{2,1,0:T(8,128)S(1)} %copy-done.2, bf16[8,256,256]{2,1,0:T(8,128)(2,1)S(1)} %get-tuple-element.11.high_ref, ...), custom_call_target="tpu_custom_call" | custom-call | tf_op jit(solution)/shard_map/pallas_call | solution.py:274
  147.7 12.9 %all_to_all.27 = f32[64,1,128]{2,1,0:T(1,128)S(1)} all-to-all(f32[64,1,128]{2,1,0:T(1,128)S(1)} %bitcast.16), channel_id=1, replica_groups=mesh['row_0'=8,'row_1'=2,'row_2'=2,'col_0'=4,'col_1'=4] {'row_1','row_2'..., dimensions={0} | all-to-all | bytes 65536 | tf_op jit(solution)/shard_map/all_to_all | solution.py:285
  160.6 0.1 reduce_sum.18
  160.7 9.5 %all_to_all.28 = f32[8,1,128]{2,1,0:T(1,128)S(1)} all-to-all(f32[8,1,128]{2,1,0:T(1,128)S(1)} %broadcast_in_dim.2), channel_id=1, replica_groups=mesh['row_0'=8,'row_1'=2,'row_2'=2,'col_0'=4,'col_1'=4] {'row_0'}, dimensions={0} | all-to-all | bytes 8192 | tf_op jit(solution)/shard_map/all_to_all | solution.py:285
  170.3 0.5 sqrt_multiply_fusion
  (2 shorter events, 0.0 us)
Async XLA Ops:
  5.3 89.7 %copy-start.3 = (f32[16,16]{1,0:T(8,128)S(1)}, f32[16,16]{1,0:T(8,128)}, u32[]{:S(2)}) copy-start(f32[16,16]{1,0:T(8,128)} %z_ref.1) | copy-start | bytes 3076
  98.6 47.0 %copy-start = (f32[1,64,2048]{2,1,0:T(8,128)S(1)}, f32[1,64,2048]{2,1,0:T(8,128)}, u32[]{:S(2)}) copy-start(f32[1,64,2048]{2,1,0:T(8,128)} %old_ref.1) | copy-start | bytes 1572868
  98.7 47.0 %copy-start.1 = (s32[1,64,2048]{2,1,0:T(8,128)S(1)}, s32[1,64,2048]{2,1,0:T(8,128)}, u32[]{:S(2)}) copy-start(s32[1,64,2048]{2,1,0:T(8,128)} %seeds_ref.1) | copy-start | bytes 1572868
  98.7 47.0 %copy-start.2 = (s32[1,64,2048]{2,1,0:T(8,128)S(1)}, s32[1,64,2048]{2,1,0:T(8,128)}, u32[]{:S(2)}) copy-start(s32[1,64,2048]{2,1,0:T(8,128)} %irreversible_ref.1) | copy-start | bytes 1572868

commit v4 on v3

--- a/solution.py
+++ b/solution.py
@@ -115,6 +115,14 @@
     return iota((count, 2 * HALF), 1) < HALF
 
 
+def odd_rows():
+    return lax.axis_index(ROW[-1]) == 1
+
+
+def swap(odd, one, two):
+    return jnp.where(odd, two, one), jnp.where(odd, one, two)
+
+
 def send_pair(out_ref, flat_ref, stacked, first, stride):
     chunks = out_ref.shape[0] // stride
     for t in range(0, 4 * chunks, 128):
@@ -130,7 +138,7 @@
         flat_ref[t : t + 128, :] = doubled[:, t : t + 128].T
     for i in range(2):
         out_ref[pl.ds(first + i, chunks, stride=stride), :] = jnp.where(
-            low_half(chunks),
+            low_half(chunks) != odd_rows(),
             flat_ref[pl.ds(i, chunks, stride=4), :],
             flat_ref[pl.ds(i + 2, chunks, stride=4), :],
         )
@@ -143,8 +151,8 @@
     for j in range(rows // 2):
         even = in_ref[pl.ds(2 * j * stride * planes + at, planes, stride=stride), :]
         odd = in_ref[pl.ds((2 * j + 1) * stride * planes + at, planes, stride=stride), :]
-        ones.append(jnp.where(low, even, pltpu.roll(odd, HALF, 1)))
-        twos.append(jnp.where(low, pltpu.roll(even, HALF, 1), odd))
+        ones.append(jnp.where(low, even, odd))
+        twos.append(pltpu.roll(jnp.where(low, odd, even), HALF, 1))
     return jnp.concatenate(ones, axis=1), jnp.concatenate(twos, axis=1)
 
 
@@ -153,12 +161,12 @@
     low = low_half(planes)
     for j in range(rows // 2):
         one = ones[:, j * 128 : (j + 1) * 128]
-        two = twos[:, j * 128 : (j + 1) * 128]
+        two = pltpu.roll(twos[:, j * 128 : (j + 1) * 128], HALF, 1)
         out_ref[pl.ds(2 * j * stride * planes + at, planes, stride=stride), :] = jnp.where(
-            low, one, pltpu.roll(two, HALF, 1)
+            low, one, two
         )
         out_ref[pl.ds((2 * j + 1) * stride * planes + at, planes, stride=stride), :] = jnp.where(
-            low, pltpu.roll(one, HALF, 1), two
+            low, two, one
         )
 
 
@@ -195,24 +203,26 @@
     energy_ref, old_ref, seeds_ref, irreversible_ref, inverses_ref, flat_refs, sems,
 ):
     pairs = [
-        (inverses_hbm, inverses_ref), (old_hbm, old_ref), (seeds_hbm, seeds_ref),
-        (energy_hbm, energy_ref), (irreversible_hbm, irreversible_ref),
+        (old_hbm, old_ref), (seeds_hbm, seeds_ref), (irreversible_hbm, irreversible_ref),
+        (energy_hbm, energy_ref), (inverses_hbm, inverses_ref),
     ]
     copies = [pltpu.make_async_copy(src, dst, sems.at[i]) for i, (src, dst) in enumerate(pairs)]
     for copy in copies:
         copy.start()
-    copies[0].wait()
-    split_inverses(inverses_ref, high_ref, low_ref, ends_ref)
-    for copy in copies[1:]:
+    for copy in copies[:4]:
         copy.wait()
     damage = jnp.where(seeds_ref[0] == 1, 1.0, old_ref[0])
+    lower = bound(old_ref[0], seeds_ref[0], irreversible_ref[0])
     energy = energy_ref[0]
     partial_value = energy - (1.0 + energy) * damage + KAPPA * lane_lap(damage)
+    send_pair(out_ref, flat_refs.at[0], jnp.concatenate(swap(odd_rows(), damage, lower), axis=0), 4, 10)
+    copies[4].wait()
+    send_single(out_ref, flat_refs.at[1], energy, 8, 10)
+    split_inverses(inverses_ref, high_ref, low_ref, ends_ref)
     solved = line_solve(jnp.concatenate([partial_value, damage], axis=0), high_ref, low_ref, ends_ref)
-    lower = bound(old_ref[0], seeds_ref[0], irreversible_ref[0])
-    send_pair(out_ref, flat_refs.at[0], jnp.concatenate([damage, lower], axis=0), 4, 10)
-    send_single(out_ref, flat_refs.at[1], energy, 8, 10)
-    send_pair(out_ref, flat_refs.at[2], solved, 0, 10)
+    count = damage.shape[0]
+    stacked = jnp.concatenate(swap(odd_rows(), solved[:count], solved[count:]), axis=0)
+    send_pair(out_ref, flat_refs.at[2], stacked, 0, 10)
 
 
 def cross_kernel(in_ref, high_ref, low_ref, ends_ref, z_ref, out_ref, change_ref):
@@ -246,7 +256,7 @@
 ):
     chunks = in_ref.shape[0] // 5
     edges = in_ref[pl.ds(4, chunks, stride=5), :]
-    inner = low_half(chunks) & (iota((chunks, 128), 0) < chunks - 1)
+    inner = (low_half(chunks) != odd_rows()) & (iota((chunks, 128), 0) < chunks - 1)
     steps = pltpu.roll(edges, chunks - 1, 0) - pltpu.roll(edges, HALF, 1)
     steps = jnp.where(inner, KAPPA * steps, 0.0)
     for i in range(4):
@@ -259,6 +269,7 @@
     tiles = [flat_ref[t : t + 128, :].T for t in range(0, 4 * chunks, 128)]
     turned = jnp.concatenate([tile[:HALF] for tile in tiles], axis=1)
     damage = jnp.concatenate([tile[HALF:] for tile in tiles], axis=1)
+    turned, damage = swap(odd_rows(), turned, damage)
     update = STEP * line_solve(turned, high_ref, low_ref, ends_ref)
     renewed = clamp(damage, update, bound(old_ref[0], seeds_ref[0], irreversible_ref[0]))
     damage_ref[0] = renewed
@@ -273,7 +284,7 @@
         args = [pltpu.with_memory_space_constraint(arg, pltpu.HBM) for arg in args]
     return pl.pallas_call(
         kernel,
-        out_shape=[jax.ShapeDtypeStruct(shape, dtype) for shape, dtype in outs],
+        out_shape=[pltpu.VMEM(shape, dtype) for shape, dtype in outs],
         in_specs=[pl.BlockSpec(memory_space=space) for _ in args],
         out_specs=[pl.BlockSpec(memory_space=pltpu.VMEM) for _ in outs],
         scratch_shapes=scratch,

time: 171 us -> 171 us (level)
  blocking collectives: 159 us -> 150 us
  waiting for transfers between devices: 0 us -> 5.68 us
  starting transfers between devices: 0 us -> 3.29 us
    all_to_all x4 -> x3, blocking collectives: 159 us -> 150 us  [exchange(): return lax.all_to_all(rows, axes, split_axis=0, concat_axis=0, tiled=True)]
    all_to_all x0 -> x1, waiting for transfers between devices: none -> 5.68 us  [exchange(): return lax.all_to_all(rows, axes, split_axis=0, concat_axis=0, tiled=True)]
    all_to_all x0 -> x1, starting transfers between devices: none -> 3.29 us  [exchange(): return lax.all_to_all(rows, axes, split_axis=0, concat_axis=0, tiled=True)]
  transfers between devices with their start and end apart: 0 -> 1, of which waited for: 0 -> 1; matrix products, arithmetic and copies ran while one was open for 0% -> 0% of each run, Pallas kernels for 0% -> 0%
where the time goes in v4:
time: 171 us; the launch traced here: 170 us
  blocking collectives  150 us (88%)
  Pallas kernels  9.16 us (5%)
  waiting for transfers between devices  5.68 us (3%)
  starting transfers between devices  3.29 us (2%)
    all_to_all x3, blocking collectives, exchange(): return lax.all_to_all(rows, axes, split_axis=0, concat_axis=0, tiled=True)  150 us
    pallas_call x3, Pallas kernels, call(): pl.pallas_call(kernel, out_shape=[pltpu.VMEM(shape, dtype) for shape, dty...  9.16 us
    all_to_all x1, waiting for transfers between devices, exchange(): return lax.all_to_all(rows, axes, split_axis=0, concat_axis=0, tiled=True)  5.68 us
  transfers between devices with their start and end apart: 1, of which 1 were waited for; matrix products, arithmetic and copies ran while one was open for 0% of the time, Pallas kernels for 0%

profile of v4, /device:TPU:1, one launch (start us, length us, event | category | flops | bytes accessed | tf_op | source)
XLA Modules:
  0.0 170.4 jit_solution(923206471223900392)
XLA Ops:
  0.6 4.4 %shard_map.77 = (f32[5120,128]{1,0:T(8,128)S(1)}, bf16[8,256,256]{2,1,0:T(8,128)(2,1)S(1)}, bf16[8,256,256]{2,1,0:T(8,128)(2,1)S(1)}, f32[8,8,256]{2,1,0:T(8,128)S(1)}) custom-call(f32[1,64,2048]{2,1,0:T(8,128)} %energy_hbm.1, f32[1,64,2048]{2,1,0:T(8,128)} %old_ref.1, s32[1,64,2048]{2,1,0:T(8,128)} %seeds_ref.1, s32[1,64,2048]{2,1,0:T(8,128)} %irreversible_ref.1, ...), custom_call_target="tpu_custom_call" | custom-call | tf_op jit(solution)/shard_map/pallas_call | solution.py:285
  5.0 0.0 copy-start.3
  5.0 89.7 %all_to_all.25 = f32[5120,1,128]{2,1,0:T(1,128)S(1)} all-to-all(f32[5120,1,128]{2,1,0:T(1,128)S(1)} %bitcast.14), channel_id=1, replica_groups=mesh['row_0'=8,'row_1'=2,'row_2'=2,'col_0'=4,'col_1'=4] {'row_0','row_1'..., dimensions={0} | all-to-all | bytes 5242880 | tf_op jit(solution)/shard_map/all_to_all | solution.py:296
  94.7 0.0 copy-done.3
  94.7 3.3 %shard_map.78 = (f32[2560,128]{1,0:T(8,128)S(1)}, f32[1,128]{1,0:T(1,128)S(1)}) custom-call(f32[5120,128]{1,0:T(8,128)S(1)} %bitcast.12, bf16[8,256,256]{2,1,0:T(8,128)(2,1)S(1)} %get-tuple-element.11.high_ref, bf16[8,256,256]{2,1,0:T(8,128)(2,1)S(1)} %get-tuple-element.12.low_ref, f32[8,8,256]{2,1,0:T(8,128)S(1)} %get-tuple-element.13.ends_ref, ...), custom_call_target="tpu_custom_call" | custom-call | tf_op jit(solution)/shard_map/pallas_call | solution.py:285
  98.0 0.0 copy-start
  98.0 0.0 copy-start.1
  98.0 0.0 copy-start.2
  98.1 46.9 %all_to_all.26 = f32[2560,1,128]{2,1,0:T(1,128)S(1)} all-to-all(f32[2560,1,128]{2,1,0:T(1,128)S(1)} %bitcast.15), channel_id=1, replica_groups=mesh['row_0'=8,'row_1'=2,'row_2'=2,'col_0'=4,'col_1'=4] {'row_0','row_1'..., dimensions={0} | all-to-all | bytes 2621440 | tf_op jit(solution)/shard_map/all_to_all | solution.py:296
  145.0 0.0 copy-done
  145.0 0.0 copy-done.1
  145.0 0.0 copy-done.2
  145.0 1.5 shard_map.79
  146.5 12.9 %all_to_all.27 = f32[64,1,128]{2,1,0:T(1,128)S(1)} all-to-all(f32[64,1,128]{2,1,0:T(1,128)S(1)} %bitcast.16), channel_id=1, replica_groups=mesh['row_0'=8,'row_1'=2,'row_2'=2,'col_0'=4,'col_1'=4] {'row_1','row_2'..., dimensions={0} | all-to-all | bytes 65536 | tf_op jit(solution)/shard_map/all_to_all | solution.py:296
  159.4 0.1 reduce_sum.18
  159.5 0.6 broadcast_in_dim.2
  160.1 3.3 %all-to-all-start.3 = ((f32[8,1,128]{2,1,0:T(1,128)}), f32[8,1,128]{2,1,0:T(1,128)S(1)}, u32[]{:S(2)}, u32[]{:S(2)}) async-start(f32[8,1,128]{2,1,0:T(1,128)} %broadcast_in_dim.2), calls=%async_computation.3 | async-start | bytes 8192 | tf_op jit(solution)/shard_map/all_to_all | solution.py:296
  163.4 0.8 copy.18
  164.2 5.7 %all-to-all-done.3 = f32[8,1,128]{2,1,0:T(1,128)S(1)} async-done(((f32[8,1,128]{2,1,0:T(1,128)}), f32[8,1,128]{2,1,0:T(1,128)S(1)}, u32[]{:S(2)}, u32[]{:S(2)}) %all-to-all-start.3) | async-done | bytes 4128 | tf_op jit(solution)/shard_map/all_to_all | solution.py:296
  169.9 0.5 sqrt_multiply_fusion
  (1 shorter events, 0.0 us)
Async XLA Ops:
  5.0 89.7 %copy-start.3 = (f32[16,16]{1,0:T(8,128)S(1)}, f32[16,16]{1,0:T(8,128)}, u32[]{:S(2)}) copy-start(f32[16,16]{1,0:T(8,128)} %z_ref.1) | copy-start | bytes 3076
  98.0 47.0 %copy-start = (f32[1,64,2048]{2,1,0:T(8,128)S(1)}, f32[1,64,2048]{2,1,0:T(8,128)}, u32[]{:S(2)}) copy-start(f32[1,64,2048]{2,1,0:T(8,128)} %old_ref.1) | copy-start | bytes 1572868
  98.0 47.0 %copy-start.1 = (s32[1,64,2048]{2,1,0:T(8,128)S(1)}, s32[1,64,2048]{2,1,0:T(8,128)}, u32[]{:S(2)}) copy-start(s32[1,64,2048]{2,1,0:T(8,128)} %seeds_ref.1) | copy-start | bytes 1572868
  98.0 47.0 %copy-start.2 = (s32[1,64,2048]{2,1,0:T(8,128)S(1)}, s32[1,64,2048]{2,1,0:T(8,128)}, u32[]{:S(2)}) copy-start(s32[1,64,2048]{2,1,0:T(8,128)} %irreversible_ref.1) | copy-start | bytes 1572868
  160.1 9.8 %all-to-all-start.3 = ((f32[8,1,128]{2,1,0:T(1,128)}), f32[8,1,128]{2,1,0:T(1,128)S(1)}, u32[]{:S(2)}, u32[]{:S(2)}) async-start(f32[8,1,128]{2,1,0:T(1,128)} %broadcast_in_dim.2), calls=%async_computation.3 | async-start | bytes 8192 | tf_op jit(solution)/shard_map/all_to_all | solution.py:296

commit v5 on v4

--- a/solution.py
+++ b/solution.py
@@ -10,6 +10,7 @@
 COL = ("col_0", "col_1")
 ALL = ROW + COL
 PLANE = ROW[1:] + COL
+CROSS = ROW[:-1] + COL + ROW[-1:]
 
 ITERS = 2
 
@@ -149,8 +150,9 @@
     low = low_half(planes)
     ones, twos = [], []
     for j in range(rows // 2):
-        even = in_ref[pl.ds(2 * j * stride * planes + at, planes, stride=stride), :]
-        odd = in_ref[pl.ds((2 * j + 1) * stride * planes + at, planes, stride=stride), :]
+        top = 2 * j * stride * planes + at
+        even = in_ref[pl.ds(top, planes, stride=2 * stride), :]
+        odd = in_ref[pl.ds(top + stride, planes, stride=2 * stride), :]
         ones.append(jnp.where(low, even, odd))
         twos.append(pltpu.roll(jnp.where(low, odd, even), HALF, 1))
     return jnp.concatenate(ones, axis=1), jnp.concatenate(twos, axis=1)
@@ -162,10 +164,11 @@
     for j in range(rows // 2):
         one = ones[:, j * 128 : (j + 1) * 128]
         two = pltpu.roll(twos[:, j * 128 : (j + 1) * 128], HALF, 1)
-        out_ref[pl.ds(2 * j * stride * planes + at, planes, stride=stride), :] = jnp.where(
+        top = 2 * j * stride * planes + at
+        out_ref[pl.ds(top, planes, stride=2 * stride), :] = jnp.where(
             low, one, two
         )
-        out_ref[pl.ds((2 * j + 1) * stride * planes + at, planes, stride=stride), :] = jnp.where(
+        out_ref[pl.ds(top + stride, planes, stride=2 * stride), :] = jnp.where(
             low, two, one
         )
 
@@ -297,7 +300,7 @@
 
 
 def cross(rows):
-    return exchange(rows.reshape(-1, 1, 128), ALL).reshape(rows.shape)
+    return exchange(rows.reshape(-1, 1, 128), CROSS).reshape(rows.shape)
 
 
 def local(energy, damage_old, crack_seeds, irreversible, line_inverses, z_inverse):

time: 171 us -> 171 us (level)
  no operation moved by 1% of the time
where the time goes in v5:
time: 171 us; the launch traced here: 170 us
  blocking collectives  150 us (88%)
  Pallas kernels  9.14 us (5%)
  waiting for transfers between devices  5.68 us (3%)
  starting transfers between devices  3.29 us (2%)
    all_to_all x3, blocking collectives, exchange(): return lax.all_to_all(rows, axes, split_axis=0, concat_axis=0, tiled=True)  150 us
    pallas_call x3, Pallas kernels, call(): pl.pallas_call(kernel, out_shape=[pltpu.VMEM(shape, dtype) for shape, dty...  9.14 us
    all_to_all x1, waiting for transfers between devices, exchange(): return lax.all_to_all(rows, axes, split_axis=0, concat_axis=0, tiled=True)  5.68 us
  transfers between devices with their start and end apart: 1, of which 1 were waited for; matrix products, arithmetic and copies ran while one was open for 0% of the time, Pallas kernels for 0%

profile of v5, /device:TPU:1, one launch (start us, length us, event | category | flops | bytes accessed | tf_op | source)
XLA Modules:
  0.0 170.4 jit_solution(8606742324190298678)
XLA Ops:
  0.6 4.4 %shard_map.77 = (f32[5120,128]{1,0:T(8,128)S(1)}, bf16[8,256,256]{2,1,0:T(8,128)(2,1)S(1)}, bf16[8,256,256]{2,1,0:T(8,128)(2,1)S(1)}, f32[8,8,256]{2,1,0:T(8,128)S(1)}) custom-call(f32[1,64,2048]{2,1,0:T(8,128)} %energy_hbm.1, f32[1,64,2048]{2,1,0:T(8,128)} %old_ref.1, s32[1,64,2048]{2,1,0:T(8,128)} %seeds_ref.1, s32[1,64,2048]{2,1,0:T(8,128)} %irreversible_ref.1, ...), custom_call_target="tpu_custom_call" | custom-call | tf_op jit(solution)/shard_map/pallas_call | solution.py:288
  5.0 0.0 copy-start.3
  5.0 87.4 %all_to_all.25 = f32[5120,1,128]{2,1,0:T(1,128)S(1)} all-to-all(f32[5120,1,128]{2,1,0:T(1,128)S(1)} %bitcast.14), channel_id=1, replica_groups=mesh['row_0'=8,'row_1'=2,'row_2'=2,'col_0'=4,'col_1'=4] {'row_0','row_1'..., dimensions={0} | all-to-all | bytes 5242880 | tf_op jit(solution)/shard_map/all_to_all | solution.py:299
  92.5 0.0 copy-done.3
  92.5 3.3 %shard_map.78 = (f32[2560,128]{1,0:T(8,128)S(1)}, f32[1,128]{1,0:T(1,128)S(1)}) custom-call(f32[5120,128]{1,0:T(8,128)S(1)} %bitcast.12, bf16[8,256,256]{2,1,0:T(8,128)(2,1)S(1)} %get-tuple-element.11.high_ref, bf16[8,256,256]{2,1,0:T(8,128)(2,1)S(1)} %get-tuple-element.12.low_ref, f32[8,8,256]{2,1,0:T(8,128)S(1)} %get-tuple-element.13.ends_ref, ...), custom_call_target="tpu_custom_call" | custom-call | tf_op jit(solution)/shard_map/pallas_call | solution.py:288
  95.7 0.0 copy-start
  95.7 0.0 copy-start.1
  95.8 0.0 copy-start.2
  95.8 47.2 %all_to_all.26 = f32[2560,1,128]{2,1,0:T(1,128)S(1)} all-to-all(f32[2560,1,128]{2,1,0:T(1,128)S(1)} %bitcast.15), channel_id=1, replica_groups=mesh['row_0'=8,'row_1'=2,'row_2'=2,'col_0'=4,'col_1'=4] {'row_0','row_1'..., dimensions={0} | all-to-all | bytes 2621440 | tf_op jit(solution)/shard_map/all_to_all | solution.py:299
  142.9 0.0 copy-done
  143.0 0.0 copy-done.1
  143.0 0.0 copy-done.2
  143.0 1.5 shard_map.79
  144.5 14.9 %all_to_all.27 = f32[64,1,128]{2,1,0:T(1,128)S(1)} all-to-all(f32[64,1,128]{2,1,0:T(1,128)S(1)} %bitcast.16), channel_id=1, replica_groups=mesh['row_0'=8,'row_1'=2,'row_2'=2,'col_0'=4,'col_1'=4] {'row_1','row_2'..., dimensions={0} | all-to-all | bytes 65536 | tf_op jit(solution)/shard_map/all_to_all | solution.py:299
  159.4 0.1 reduce_sum.18
  159.4 0.6 broadcast_in_dim.2
  160.0 3.3 %all-to-all-start.3 = ((f32[8,1,128]{2,1,0:T(1,128)}), f32[8,1,128]{2,1,0:T(1,128)S(1)}, u32[]{:S(2)}, u32[]{:S(2)}) async-start(f32[8,1,128]{2,1,0:T(1,128)} %broadcast_in_dim.2), calls=%async_computation.3 | async-start | bytes 8192 | tf_op jit(solution)/shard_map/all_to_all | solution.py:299
  163.3 0.8 copy.18
  164.1 5.7 %all-to-all-done.3 = f32[8,1,128]{2,1,0:T(1,128)S(1)} async-done(((f32[8,1,128]{2,1,0:T(1,128)}), f32[8,1,128]{2,1,0:T(1,128)S(1)}, u32[]{:S(2)}, u32[]{:S(2)}) %all-to-all-start.3) | async-done | bytes 4128 | tf_op jit(solution)/shard_map/all_to_all | solution.py:299
  169.8 0.5 sqrt_multiply_fusion
  (1 shorter events, 0.0 us)
Async XLA Ops:
  5.0 87.4 %copy-start.3 = (f32[16,16]{1,0:T(8,128)S(1)}, f32[16,16]{1,0:T(8,128)}, u32[]{:S(2)}) copy-start(f32[16,16]{1,0:T(8,128)} %z_ref.1) | copy-start | bytes 3076
  95.7 47.2 %copy-start = (f32[1,64,2048]{2,1,0:T(8,128)S(1)}, f32[1,64,2048]{2,1,0:T(8,128)}, u32[]{:S(2)}) copy-start(f32[1,64,2048]{2,1,0:T(8,128)} %old_ref.1) | copy-start | bytes 1572868
  95.7 47.2 %copy-start.1 = (s32[1,64,2048]{2,1,0:T(8,128)S(1)}, s32[1,64,2048]{2,1,0:T(8,128)}, u32[]{:S(2)}) copy-start(s32[1,64,2048]{2,1,0:T(8,128)} %seeds_ref.1) | copy-start | bytes 1572868
  95.8 47.2 %copy-start.2 = (s32[1,64,2048]{2,1,0:T(8,128)S(1)}, s32[1,64,2048]{2,1,0:T(8,128)}, u32[]{:S(2)}) copy-start(s32[1,64,2048]{2,1,0:T(8,128)} %irreversible_ref.1) | copy-start | bytes 1572868
  160.0 9.8 %all-to-all-start.3 = ((f32[8,1,128]{2,1,0:T(1,128)}), f32[8,1,128]{2,1,0:T(1,128)S(1)}, u32[]{:S(2)}, u32[]{:S(2)}) async-start(f32[8,1,128]{2,1,0:T(1,128)} %broadcast_in_dim.2), calls=%async_computation.3 | async-start | bytes 8192 | tf_op jit(solution)/shard_map/all_to_all | solution.py:299
